TPU v7x, 32 devices: a whole 2x2x4 slice. The times are simulated.
32 devices in a mesh: atoms: 16 (over z, y, x), chan: 2 (over core).
Axes of the slice: x: 2, y: 2, z: 4, core: 2. Of those that a mesh axis runs over, the one named last changes fastest.
Arguments:
- features: bfloat16 [128, 8192], P('chan', 'atoms'), may hold values from -6 to 6
- positions: float32 [3, 8192], P(None, 'atoms'), may hold values from 0 to 256
- block_counts: int32 [64], P('atoms'), may hold values from 64 to 128
- radial_w: float32 [8, 3, 128], P(None, None, 'chan'), may hold values from -2 to 2
- mix_w: bfloat16 [4, 128, 128], replicated, may hold values from -0.25 to 0.25
- read_w: float32 [128], P('chan'), may hold values from -0.5 to 0.5
- ghost_lists: int32 [16, 2, 2], P('atoms'), may hold values from 0 to 3, as said below
- tile_pairs: int32 [16, 24, 2], P('atoms'), may hold values from 0 to 7, as said below
- tile_count: int32 [16], P('atoms'), may hold values from 9 to 24, as said below
Outputs:
- updated: bfloat16 [128, 8192], P('chan', 'atoms')
- energies: float32 [8192], P('atoms')
- scale: float32 [], replicated
Inputs may be any that keep to these rules, and one draw needn't show every extreme that they name: `ghost_lists`: row 0 of group g lists each of its even-numbered blocks once and row 1 each odd-numbered block once, in some order. `tile_pairs`: codes below 4 name the group's own block, codes 4 to 5 a slot of the previous group's ghost_lists row 1, higher codes a slot of the next group's row 0; no code points outside the first or last group. Tile t < 4 of each group is (t, t). Tiles from tile_count[g] on are (0, 0). `tile_count`: some group has 24 live tiles.
All inputs are finite; a program needn't handle non-finite values.
Results may differ from a plain program's by a relative error of at most 0.007.
Values may be sent and summed in bfloat16 or wider, within the bound.
A program may use at most 64 MiB of HBM per device.

v0:
```python
import jax
import jax.numpy as jnp
from jax import lax
from jax.sharding import PartitionSpec as P

NR = 8


root_three = 3.0**0.5
root_fifteen = 15.0**0.5
half_root_five = 0.5 * 5.0**0.5
half_root_fifteen = 0.5 * 15.0**0.5
cutoff_square = 9.0
soften = 0.25
center_step = 3.0 / 7.0
radial_sharp = 2.0
tiles_per_turn = 4


def extended(block, sides, width):
    for axis, dim in sides:
        count = lax.axis_size(axis)
        forward = [(i, i + 1) for i in range(count - 1)]
        backward = [(target, source) for source, target in forward]
        low = lax.ppermute(
            lax.slice_in_dim(block, block.shape[dim] - width, None, axis=dim), axis, forward
        )
        high = lax.ppermute(lax.slice_in_dim(block, 0, width, axis=dim), axis, backward)
        block = jnp.concatenate([low, block, high], axis=dim)
    return block


def harmonics(unit_x, unit_y, unit_z):
    return jnp.stack(
        [
            jnp.ones_like(unit_x),
            root_three * unit_x,
            root_three * unit_y,
            root_three * unit_z,
            root_fifteen * unit_x * unit_y,
            root_fifteen * unit_y * unit_z,
            half_root_five * (2.0 * unit_z * unit_z - unit_x * unit_x - unit_y * unit_y),
            root_fifteen * unit_x * unit_z,
            half_root_fifteen * (unit_x * unit_x - unit_y * unit_y),
        ]
    )


def tile_kernel(pos_recv, pos_send, self_pair):
    offset = pos_send[:, None, :] - pos_recv[:, :, None]
    dist_sq = jnp.sum(offset * offset, axis=0)
    block_width = dist_sq.shape[0]
    diagonal = (
        lax.broadcasted_iota(jnp.int32, (block_width, block_width), 0)
        == lax.broadcasted_iota(jnp.int32, (block_width, block_width), 1)
    ).astype(jnp.float32)
    cutoff = jnp.square(jnp.maximum(1.0 - dist_sq / cutoff_square, 0.0)) * (
        1.0 - self_pair * diagonal
    )
    distance = jnp.sqrt(dist_sq + soften)
    unit = offset / distance
    angular = harmonics(unit[0], unit[1], unit[2]) * cutoff
    centers = jnp.arange(NR, dtype=jnp.float32) * center_step
    radial = jnp.exp(-radial_sharp * jnp.square(distance[None] - centers[:, None, None]))
    return (radial[:, None] * angular[None]).astype(jnp.bfloat16)


def tile_term(pos_recv, pos_send, sender_rows, self_pair, table):
    kernel = tile_kernel(pos_recv, pos_send, self_pair)
    partial_sums = jnp.einsum(
        "cj,kmij->ckmi", sender_rows, kernel, preferred_element_type=jnp.float32
    )
    return jnp.einsum("kmc,ckmi->cmi", table, partial_sums, precision=lax.Precision.HIGHEST)


def invariants(density):
    first = density[:, 0]
    return jnp.stack(
        [
            first,
            first * first,
            jnp.sum(jnp.square(density[:, 1:4]), axis=1),
            jnp.sum(jnp.square(density[:, 4:9]), axis=1),
        ]
    )


def per_device(
    features, positions, block_counts, radial_w, mix_w, read_w, ghost_lists, tile_pairs, tile_count
):
    local_chan = features.shape[0]
    blocks = block_counts.shape[0]
    local_atoms = positions.shape[1]
    block_width = local_atoms // blocks
    ghosts = ghost_lists.shape[2]
    present = (jnp.arange(block_width, dtype=jnp.int32)[None, :] < block_counts[:, None]).astype(
        jnp.float32
    )
    present_flat = present.reshape(-1)
    senders = (features.astype(jnp.float32) * present_flat[None, :]).astype(jnp.bfloat16)
    own_where = positions.reshape(3, blocks, block_width)
    send_lists = ghost_lists[0]
    list_row = jnp.concatenate(
        [
            send_lists.reshape(-1).astype(jnp.float32),
            jnp.zeros((local_atoms - 2 * ghosts,), jnp.float32),
        ]
    )
    place_rows = jnp.concatenate([positions, list_row[None, :]], axis=0)
    widened = extended(senders, (("atoms", 1),), local_atoms)
    wide_places = extended(place_rows, (("atoms", 1),), local_atoms)
    source_rows = widened.reshape(local_chan, 3 * blocks, block_width)
    source_where = wide_places[:3].reshape(3, 3 * blocks, block_width)
    left_list = wide_places[3, ghosts : 2 * ghosts].astype(jnp.int32)
    right_list = wide_places[3, 2 * local_atoms : 2 * local_atoms + ghosts].astype(jnp.int32)
    lookup = jnp.concatenate(
        [blocks + jnp.arange(blocks, dtype=jnp.int32), left_list, 2 * blocks + right_list]
    )
    degree = jnp.array([0, 1, 1, 1, 2, 2, 2, 2, 2], dtype=jnp.int32)
    table = jnp.take(radial_w, degree, axis=1)
    tile_list = tile_pairs[0]
    tile_total = tile_count[0]
    batched = jax.vmap(tile_term, in_axes=(1, 1, 1, 0, None))

    def one_turn(turn, totals):
        tile_ids = turn * tiles_per_turn + jnp.arange(tiles_per_turn, dtype=jnp.int32)
        receivers = tile_list[tile_ids, 0]
        codes = tile_list[tile_ids, 1]
        weights = (tile_ids < tile_total).astype(jnp.float32)
        picked = jnp.take(source_rows, lookup[codes], axis=1)
        picked_where = jnp.take(source_where, lookup[codes], axis=1)
        pos_recv = jnp.take(own_where, receivers, axis=1)
        self_pairs = ((codes < blocks) & (codes == receivers)).astype(jnp.float32)
        terms = batched(pos_recv, picked_where, picked, self_pairs, table)
        return totals.at[receivers].add(terms * weights[:, None, None, None])

    start = jnp.zeros((blocks, local_chan, 9, block_width), jnp.float32)
    turns = (tile_total + tiles_per_turn - 1) // tiles_per_turn
    totals = lax.fori_loop(0, turns, one_turn, start)
    density = totals.transpose(1, 2, 0, 3).reshape(local_chan, 9, local_atoms)
    basis = invariants(density).astype(jnp.bfloat16)
    chan_start = lax.axis_index("chan") * local_chan
    my_outputs = lax.dynamic_slice_in_dim(mix_w, chan_start, local_chan, 2)
    weights = my_outputs
    mixed = jnp.einsum(
        "qco,qca->oa",
        weights,
        lax.all_gather(basis, "chan", axis=1, tiled=True),
        preferred_element_type=jnp.float32,
    )
    hidden = features.astype(jnp.float32) + jax.nn.silu(mixed)
    updated = (hidden * present_flat[None, :]).astype(jnp.bfloat16)
    local_energy = jnp.dot(read_w, hidden, precision=lax.Precision.HIGHEST)
    energy = lax.psum(local_energy, "chan")
    total_square, total_atoms = lax.psum(
        (jnp.sum(present_flat * energy * energy), jnp.sum(present_flat)), "atoms"
    )
    scale = jnp.sqrt(1.0 + total_square / total_atoms)
    return (updated, energy * present_flat / scale, scale)


def solution(mesh):
    in_specs = (
        P("chan", "atoms"),
        P(None, "atoms"),
        P("atoms"),
        P(None, None, "chan"),
        P(),
        P("chan"),
        P("atoms", None, None),
        P("atoms", None, None),
        P("atoms"),
    )
    out_specs = (P("chan", "atoms"), P("atoms"), P())
    return jax.shard_map(
        per_device, mesh=mesh, in_specs=in_specs, out_specs=out_specs, check_vma=False
    )
```

profile of v0, /device:TPU:0, one launch (start us, length us, event | category | flops | bytes accessed | tf_op | source)
XLA Modules:
  0.0 303.8 jit_solution(6518405656221773046)
XLA Ops:
  0.6 0.8 fusion.32
  1.4 0.9 fusion.25
  2.3 4.9 %collective-permute-start.2 = (bf16[64,512]{1,0:T(8,128)(2,1)S(1)}, bf16[64,512]{1,0:T(8,128)(2,1)S(1)}, u32[]{:S(2)}, u32[]{:S(2)}) collective-permute-start(bf16[64,512]{1,0:T(8,128)(2,1)S(1)} %fusion.25), channel_id=1, source_target_pairs={{0,2},{2,4},{4,6},{6,8},{8,10},{10,12},{12,14},{14,16},{16,18},{18... | collective-permute-start | bytes 196616 | tf_op jit(solution)/shard_map/ppermute | solution.py:25
  7.1 1.3 collective-permute-start.3
  8.4 0.7 convert_element_type.63
  9.2 0.7 pad_maximum_fusion.4
  9.9 4.5 %collective-permute-start = (f32[4,512]{1,0:T(4,128)S(1)}, f32[4,512]{1,0:T(4,128)S(1)}, u32[]{:S(2)}, u32[]{:S(2)}) collective-permute-start(f32[4,512]{1,0:T(4,128)S(1)} %pad_maximum_fusion.4), channel_id=1, source_target_pairs={{0,2},{2,4},{4,6},{6,8},{8,10},{10,12},{12,14},{14,16},{16,18},{18... | collective-permute-start | bytes 24584 | tf_op jit(solution)/shard_map/ppermute | solution.py:25
  14.5 1.3 collective-permute-start.1
  15.8 1.4 convert_reduce_fusion
  18.5 1.3 gather_fusion.6
  20.4 0.7 fusion.29
  21.3 1.2 broadcast_in_dim.44
  22.5 192.0 %while.10 = (s32[]{:T(128)}, f32[4,64,9,128]{3,1,2,0:T(8,128)}, s32[]{:T(128)}, s32[24,2]{0,1:T(2,128)}, s32[8]{0:T(128)S(1)}, /*index=5*/bf16[64,12,128]{2,0,1:...) while((s32[]{:T(128)}, f32[4,64,9,128]{3,1,2,0:T(8,128)}, ...), condition=%wide.region_3.4_spmd, body=%wide.region_0.3_spmd.sunk | while | flops 647305344 | bytes 55782184 | solution.py:139
  22.5 1.3 gather_fusion
  23.8 1.3 gather_fusion.2
  25.2 1.3 gather_fusion.1
  29.2 1.7 multiply_exponential_fusion.2
  31.5 7.1 %fusion.65 = f32[4,64,8,9,128]{4,1,3,2,0:T(8,128)} fusion(f32[4,9,128,128]{3,2,1,0:T(8,128)S(1)} %broadcast_multiply_fusion.2, f32[4,8,128,128]{3,2,1,0:T(8,128)} %multiply_exponential_fusion.2, bf16[4,64,128]{2,1,0:T(8,128)(2,1)S(1)} %gather_fusion.5, pred[4]{0:T(512)(128)(4,1)S(1)} %compare_and_fusion.3), kind=kOutput, calls=%fused_computation.9.clone.1 | convolution fusion | flops 613449728 | bytes 13959172 | tf_op jit(solution)/shard_map/while/body/vmap(cj,kmij->ckmi)/dot_general | solution.py:70
  38.7 18.5 %fusion.66 = f32[64,9,1,4,128]{4,2,3,1,0:T(1,128)S(1)} fusion(f32[8,9,64,1,1]{0,3,4,1,2:T(1,128)S(1)} %copy.42, f32[4,64,8,9,128]{4,1,3,2,0:T(8,128)} %fusion.65), kind=kOutput, calls=%fused_computation.10.clone.1 | convolution fusion | flops 28311552 | bytes 10635264 | tf_op jit(solution)/shard_map/while/body/vmap(kmc,ckmi->cmi)/dot_general | solution.py:73
  57.2 0.7 compare_convert_fusion.2
  58.5 1.4 scatter_fusion
  59.9 1.0 copy-done.2
  61.0 1.3 gather_fusion
  62.3 1.3 gather_fusion.2
  63.6 1.3 gather_fusion.1
  67.6 1.7 multiply_exponential_fusion.2
  69.9 7.1 %fusion.65 = f32[4,64,8,9,128]{4,1,3,2,0:T(8,128)} fusion(f32[4,9,128,128]{3,2,1,0:T(8,128)S(1)} %broadcast_multiply_fusion.2, f32[4,8,128,128]{3,2,1,0:T(8,128)} %multiply_exponential_fusion.2, bf16[4,64,128]{2,1,0:T(8,128)(2,1)S(1)} %gather_fusion.5, pred[4]{0:T(512)(128)(4,1)S(1)} %compare_and_fusion.3), kind=kOutput, calls=%fused_computation.9.clone.1 | convolution fusion | flops 613449728 | bytes 13959172 | tf_op jit(solution)/shard_map/while/body/vmap(cj,kmij->ckmi)/dot_general | solution.py:70
  77.2 18.5 %fusion.66 = f32[64,9,1,4,128]{4,2,3,1,0:T(1,128)S(1)} fusion(f32[8,9,64,1,1]{0,3,4,1,2:T(1,128)S(1)} %copy.42, f32[4,64,8,9,128]{4,1,3,2,0:T(8,128)} %fusion.65), kind=kOutput, calls=%fused_computation.10.clone.1 | convolution fusion | flops 28311552 | bytes 10635264 | tf_op jit(solution)/shard_map/while/body/vmap(kmc,ckmi->cmi)/dot_general | solution.py:73
  95.7 0.7 compare_convert_fusion.2
  96.9 1.4 scatter_fusion
  98.3 1.0 copy-done.2
  99.4 1.3 gather_fusion
  100.7 1.3 gather_fusion.2
  102.0 1.3 gather_fusion.1
  106.0 1.7 multiply_exponential_fusion.2
  108.3 7.1 %fusion.65 = f32[4,64,8,9,128]{4,1,3,2,0:T(8,128)} fusion(f32[4,9,128,128]{3,2,1,0:T(8,128)S(1)} %broadcast_multiply_fusion.2, f32[4,8,128,128]{3,2,1,0:T(8,128)} %multiply_exponential_fusion.2, bf16[4,64,128]{2,1,0:T(8,128)(2,1)S(1)} %gather_fusion.5, pred[4]{0:T(512)(128)(4,1)S(1)} %compare_and_fusion.3), kind=kOutput, calls=%fused_computation.9.clone.1 | convolution fusion | flops 613449728 | bytes 13959172 | tf_op jit(solution)/shard_map/while/body/vmap(cj,kmij->ckmi)/dot_general | solution.py:70
  115.6 18.5 %fusion.66 = f32[64,9,1,4,128]{4,2,3,1,0:T(1,128)S(1)} fusion(f32[8,9,64,1,1]{0,3,4,1,2:T(1,128)S(1)} %copy.42, f32[4,64,8,9,128]{4,1,3,2,0:T(8,128)} %fusion.65), kind=kOutput, calls=%fused_computation.10.clone.1 | convolution fusion | flops 28311552 | bytes 10635264 | tf_op jit(solution)/shard_map/while/body/vmap(kmc,ckmi->cmi)/dot_general | solution.py:73
  134.1 0.7 compare_convert_fusion.2
  135.3 1.4 scatter_fusion
  136.7 1.0 copy-done.2
  137.7 1.3 gather_fusion
  139.1 1.3 gather_fusion.2
  140.4 1.3 gather_fusion.1
  144.4 1.7 multiply_exponential_fusion.2
  146.7 7.1 %fusion.65 = f32[4,64,8,9,128]{4,1,3,2,0:T(8,128)} fusion(f32[4,9,128,128]{3,2,1,0:T(8,128)S(1)} %broadcast_multiply_fusion.2, f32[4,8,128,128]{3,2,1,0:T(8,128)} %multiply_exponential_fusion.2, bf16[4,64,128]{2,1,0:T(8,128)(2,1)S(1)} %gather_fusion.5, pred[4]{0:T(512)(128)(4,1)S(1)} %compare_and_fusion.3), kind=kOutput, calls=%fused_computation.9.clone.1 | convolution fusion | flops 613449728 | bytes 13959172 | tf_op jit(solution)/shard_map/while/body/vmap(cj,kmij->ckmi)/dot_general | solution.py:70
  154.0 18.5 %fusion.66 = f32[64,9,1,4,128]{4,2,3,1,0:T(1,128)S(1)} fusion(f32[8,9,64,1,1]{0,3,4,1,2:T(1,128)S(1)} %copy.42, f32[4,64,8,9,128]{4,1,3,2,0:T(8,128)} %fusion.65), kind=kOutput, calls=%fused_computation.10.clone.1 | convolution fusion | flops 28311552 | bytes 10635264 | tf_op jit(solution)/shard_map/while/body/vmap(kmc,ckmi->cmi)/dot_general | solution.py:73
  172.5 0.7 compare_convert_fusion.2
  173.7 1.4 scatter_fusion
  175.1 1.0 copy-done.2
  176.2 1.3 gather_fusion
  177.5 1.3 gather_fusion.2
  178.8 1.3 gather_fusion.1
  182.8 1.7 multiply_exponential_fusion.2
  185.1 7.1 %fusion.65 = f32[4,64,8,9,128]{4,1,3,2,0:T(8,128)} fusion(f32[4,9,128,128]{3,2,1,0:T(8,128)S(1)} %broadcast_multiply_fusion.2, f32[4,8,128,128]{3,2,1,0:T(8,128)} %multiply_exponential_fusion.2, bf16[4,64,128]{2,1,0:T(8,128)(2,1)S(1)} %gather_fusion.5, pred[4]{0:T(512)(128)(4,1)S(1)} %compare_and_fusion.3), kind=kOutput, calls=%fused_computation.9.clone.1 | convolution fusion | flops 613449728 | bytes 13959172 | tf_op jit(solution)/shard_map/while/body/vmap(cj,kmij->ckmi)/dot_general | solution.py:70
  192.4 18.5 %fusion.66 = f32[64,9,1,4,128]{4,2,3,1,0:T(1,128)S(1)} fusion(f32[8,9,64,1,1]{0,3,4,1,2:T(1,128)S(1)} %copy.42, f32[4,64,8,9,128]{4,1,3,2,0:T(8,128)} %fusion.65), kind=kOutput, calls=%fused_computation.10.clone.1 | convolution fusion | flops 28311552 | bytes 10635264 | tf_op jit(solution)/shard_map/while/body/vmap(kmc,ckmi->cmi)/dot_general | solution.py:73
  210.9 0.7 compare_convert_fusion.2
  212.1 1.4 scatter_fusion
  213.5 1.0 copy-done.2
  214.6 1.4 copy_bitcast_fusion
  216.2 2.2 all_gather.3
  218.4 1.0 multiply_convert_fusion.3
  219.6 2.5 psum.21
  222.0 0.7 multiply_reduce_fusion
  222.7 77.9 %all-reduce.3 = (f32[]{:T(128)}, f32[]{:T(128)}) all-reduce(f32[]{:T(128)} %multiply_reduce_fusion, f32[]{:T(128)} %convert_reduce_fusion), channel_id=1, replica_groups=mesh['atoms'=16,'chan'=2] {'atoms'}, use_global_device_ids=true, to_apply=%region_8.9 | all-reduce | flops 2 | bytes 16 | tf_op jit(solution)/shard_map/psum | solution.py:155
  (198 shorter events, 22.1 us)
Async XLA Ops:
  0.6 217.8 %copy-start = (bf16[4,128,128]{2,1,0:T(8,128)(2,1)S(1)}, bf16[4,128,128]{2,1,0:T(8,128)(2,1)}, u32[]{:S(2)}) copy-start(bf16[4,128,128]{2,1,0:T(8,128)(2,1)} %param.16) | copy-start | bytes 393220
  2.3 19.0 %collective-permute-start.2 = (bf16[64,512]{1,0:T(8,128)(2,1)S(1)}, bf16[64,512]{1,0:T(8,128)(2,1)S(1)}, u32[]{:S(2)}, u32[]{:S(2)}) collective-permute-start(bf16[64,512]{1,0:T(8,128)(2,1)S(1)} %fusion.25), channel_id=1, source_target_pairs={{0,2},{2,4},{4,6},{6,8},{8,10},{10,12},{12,14},{14,16},{16,18},{18... | collective-permute-start | bytes 196616 | tf_op jit(solution)/shard_map/ppermute | solution.py:25
  7.1 14.1 %collective-permute-start.3 = (bf16[64,512]{1,0:T(8,128)(2,1)S(1)}, bf16[64,512]{1,0:T(8,128)(2,1)S(1)}, u32[]{:S(2)}, u32[]{:S(2)}) collective-permute-start(bf16[64,512]{1,0:T(8,128)(2,1)S(1)} %fusion.25), channel_id=1, source_target_pairs={{2,0},{4,2},{6,4},{8,6},{10,8},{12,10},{14,12},{16,14},{18,16},{20... | collective-permute-start | bytes 196616 | tf_op jit(solution)/shard_map/ppermute | solution.py:28
  9.9 10.5 %collective-permute-start = (f32[4,512]{1,0:T(4,128)S(1)}, f32[4,512]{1,0:T(4,128)S(1)}, u32[]{:S(2)}, u32[]{:S(2)}) collective-permute-start(f32[4,512]{1,0:T(4,128)S(1)} %pad_maximum_fusion.4), channel_id=1, source_target_pairs={{0,2},{2,4},{4,6},{6,8},{8,10},{10,12},{12,14},{14,16},{16,18},{18... | collective-permute-start | bytes 24584 | tf_op jit(solution)/shard_map/ppermute | solution.py:25
  14.5 5.9 %collective-permute-start.1 = (f32[4,512]{1,0:T(4,128)S(1)}, f32[4,512]{1,0:T(4,128)S(1)}, u32[]{:S(2)}, u32[]{:S(2)}) collective-permute-start(f32[4,512]{1,0:T(4,128)S(1)} %pad_maximum_fusion.4), channel_id=1, source_target_pairs={{2,0},{4,2},{6,4},{8,6},{10,8},{12,10},{14,12},{16,14},{18,16},{20... | collective-permute-start | bytes 24584 | tf_op jit(solution)/shard_map/ppermute | solution.py:28
  57.2 1.3 copy-start.1
  59.9 1.0 copy-start.2
  95.7 1.3 copy-start.1
  98.3 1.0 copy-start.2
  134.1 1.3 copy-start.1
  136.7 1.0 copy-start.2
  172.4 1.3 copy-start.1
  175.1 1.0 copy-start.2
  210.8 1.3 copy-start.1
  213.5 1.0 copy-start.2
  214.6 3.9 %copy-start.3 = (bf16[64,512]{1,0:T(8,128)(2,1)S(1)}, bf16[64,512]{1,0:T(8,128)(2,1)}, u32[]{:S(2)}) copy-start(bf16[64,512]{1,0:T(8,128)(2,1)} %param.12) | copy-start | bytes 196612
  216.0 3.4 %copy-start.5 = (f32[64]{0:T(128)S(1)}, f32[64]{0:T(128)}, u32[]{:S(2)}) copy-start(f32[64]{0:T(128)} %param.17) | copy-start | bytes 772
  216.0 6.0 %copy-start.4 = (s32[4]{0:T(128)S(1)}, s32[4]{0:T(128)}, u32[]{:S(2)}) copy-start(s32[4]{0:T(128)} %param.14) | copy-start | bytes 52
where the time goes:
time: 307 us; the launch traced here: 304 us
  matrix products  129 us (42%)
  blocking collectives  82.6 us (27%)
  local copies, waits for them, and re-layouts  40.1 us (13%)
  other arithmetic  34.7 us (11%)
  starting transfers between devices  12 us (4%)
  between operations  3.98 us (1%)
    dot_general x5, matrix products, tile_term(): jnp.einsum('kmc,ckmi->cmi', table, partial_sums, precision=lax.Precision....  92.3 us
    psum x1, blocking collectives, per_device(): lax.psum((jnp.sum(present_flat * energy * energy), jnp.sum(present_flat))...  77.9 us
    dot_general x5, matrix products, tile_term(): jnp.einsum('cj,kmij->ckmi', sender_rows, kernel, preferred_element_type=j...  35.3 us
    ppermute x2, starting transfers between devices, extended(): lax.ppermute(lax.slice_in_dim(block, block.shape[dim] - width, None, axis...  9.41 us
    exp x5, other arithmetic, tile_kernel(): jnp.exp(-radial_sharp * jnp.square(distance[None] - centers[:, None, None]))  8.63 us
    scatter-add x5, other arithmetic, one_turn(): return totals.at[receivers].add(terms * weights[:, None, None, None])  6.87 us
    while x25, local copies, waits for them, and re-layouts  6.78 us
    gather x5, local copies, waits for them, and re-layouts, one_turn(): codes = tile_list[tile_ids, 1]  6.62 us
  transfers between devices with their start and end apart: 4, of which 1 were waited for; matrix products, arithmetic and copies ran while one was open for 2% of the time, Pallas kernels for 0%

commit v1 on v0

v1 whole, which is shorter than its diff:
```python
import functools

import jax
import jax.numpy as jnp
from jax import lax
from jax.experimental import pallas as pl
from jax.experimental.pallas import tpu as pltpu
from jax.sharding import PartitionSpec as P

root_three = 3.0**0.5
root_fifteen = 15.0**0.5
half_root_five = 0.5 * 5.0**0.5
half_root_fifteen = 0.5 * 15.0**0.5
cutoff_square = 9.0
soften = 0.25
center_step = 3.0 / 7.0
radial_sharp = 2.0
degrees = ((0,), (1, 2, 3), (4, 5, 6, 7, 8))
MESH = pl.DeviceIdType.MESH


def gather_kernel(
    shape, blocks, feat_ref, place_ref, w_ref, feats, places, walls, sems_s, sems_r, local_sems
):
    groups, peers = shape
    g, h = lax.axis_index("atoms"), lax.axis_index("chan")
    chans, width = feat_ref.shape[0], feat_ref.shape[1] // blocks
    after, before = lax.rem(g + 1, groups), lax.rem(g + groups - 1, groups)
    barrier = pltpu.get_barrier_semaphore()
    for d in range(1, peers):
        pl.semaphore_signal(
            barrier, inc=1, device_id=(g, lax.rem(h + d, peers)), device_id_type=MESH
        )
    for there in (after, before):
        for d in range(peers):
            pl.semaphore_signal(
                barrier, inc=1, device_id=(there, lax.rem(h + d, peers)), device_id_type=MESH
            )
    rows = pl.ds(pl.multiple_of(h * chans, chans), chans)
    own = pl.ds(0, blocks * width)
    locals_ = [
        pltpu.make_async_copy(feat_ref, feats.at[rows, own], local_sems.at[0]),
        pltpu.make_async_copy(w_ref, walls.at[h], local_sems.at[1]),
    ]
    for copy in locals_:
        copy.start()
    pl.semaphore_wait(barrier, 3 * peers - 1)
    copies = []

    def send(src, dst, device):
        slot = len(copies)
        copy = pltpu.make_async_remote_copy(
            src_ref=src,
            dst_ref=dst,
            send_sem=sems_s.at[slot],
            recv_sem=sems_r.at[slot],
            device_id=device,
            device_id_type=MESH,
        )
        copy.start()
        copies.append(copy)

    half = blocks // 2
    for d in range(peers):
        to = lax.rem(h + d, peers)
        for n in range(half):
            for there, block, slot in (
                (after, 2 * n + 1, blocks + n),
                (before, 2 * n, blocks + half + n),
            ):
                send(
                    feat_ref.at[:, pl.ds(block * width, width)],
                    feats.at[rows, pl.ds(slot * width, width)],
                    (there, to),
                )
    send(place_ref, places.at[0], (after, h))
    send(place_ref, places.at[1], (before, h))
    for d in range(1, peers):
        to = (g, lax.rem(h + d, peers))
        send(feat_ref, feats.at[rows, own], to)
        send(w_ref, walls.at[h], to)
    for copy in locals_:
        copy.wait()
    for copy in copies:
        copy.wait()


def compute_kernel(
    peers, blocks, basis_count, pairs, count, feats, place, places, walls, mix, upd, stats,
    table, spos, rpos, feat_rows, acc,
):
    h = lax.axis_index("chan")
    width = feats.shape[1] // (2 * blocks)
    part = width // peers
    half = blocks // 2
    mine = pl.ds(pl.multiple_of(h * part, part), part)
    w = jnp.concatenate([walls[n] for n in range(peers)], axis=1)
    atom = lax.broadcasted_iota(jnp.int32, (width, 1), 0).astype(jnp.float32)

    def block_of(slot):
        return feats[:, slot * width : (slot + 1) * width].astype(jnp.float32)

    def store_source(code, rows, present):
        masked = jnp.where(atom < present, rows, 0.0)
        for l in range(3):
            for k in range(basis_count):
                table[code, l, k * width : (k + 1) * width, :] = (
                    masked * w[3 * k + l : 3 * k + l + 1, :]
                ).astype(jnp.bfloat16)

    for b in range(blocks):
        rows = block_of(b).T
        feat_rows[b] = rows
        store_source(b, rows, place[3:4, b : b + 1])
        spos[b] = place[:, b * width : (b + 1) * width]
        for axis in range(3):
            rpos[3 * b + axis] = jnp.broadcast_to(
                place[axis : axis + 1, b * width : (b + 1) * width], (width, width)
            ).T
    for side in range(2):
        near = places.at[side]
        for n in range(half):
            column = blocks + (1 - side) * half + n
            listed = near[3:4, column : column + 1]
            code = blocks + side * half + n
            rows, where, present = None, None, None
            for m in range(half):
                block = 2 * m + 1 - side
                is_it = listed == float(block)
                new = (
                    block_of(blocks + side * half + m),
                    near[:, block * width : (block + 1) * width],
                    near[3:4, block : block + 1],
                )
                if m == 0:
                    rows, where, present = new
                else:
                    rows = jnp.where(is_it, new[0], rows)
                    where = jnp.where(is_it, new[1], where)
                    present = jnp.where(is_it, new[2], present)
            store_source(code, rows.T, present)
            spos[code] = where
    acc[...] = jnp.zeros_like(acc)
    diagonal = (
        lax.broadcasted_iota(jnp.int32, (part, width), 0) + h * part
        == lax.broadcasted_iota(jnp.int32, (part, width), 1)
    ).astype(jnp.float32)

    def one_tile(t, carry):
        r, q = pairs[0, t, 0], pairs[0, t, 1]
        dx = spos[q, 0:1, :] - rpos[3 * r, mine, :]
        dy = spos[q, 1:2, :] - rpos[3 * r + 1, mine, :]
        dz = spos[q, 2:3, :] - rpos[3 * r + 2, mine, :]
        d2 = dx * dx + dy * dy + dz * dz
        is_self = (r == q).astype(jnp.float32)
        edge = jnp.maximum(1.0 - d2 * (1.0 / cutoff_square), 0.0)
        cut = edge * edge * (1.0 - is_self * diagonal)
        inverse = lax.rsqrt(d2 + soften)
        dist = (d2 + soften) * inverse
        x, y, z = dx * inverse, dy * inverse, dz * inverse
        cx, cy = cut * root_fifteen * x, cut * root_fifteen * y
        cut3 = cut * root_three
        angular = (
            cut,
            cut3 * x,
            cut3 * y,
            cut3 * z,
            cx * y,
            cy * z,
            cut * half_root_five * (2.0 * z * z - x * x - y * y),
            cx * z,
            cut * half_root_fifteen * (x * x - y * y),
        )
        radial = []
        for k in range(basis_count):
            off = dist - center_step * k
            radial.append(jnp.exp(-radial_sharp * off * off))
        for l, ms in enumerate(degrees):
            lhs = jnp.concatenate(
                [
                    jnp.concatenate(
                        [(radial[k] * angular[m]).astype(jnp.bfloat16) for k in range(basis_count)],
                        axis=1,
                    )
                    for m in ms
                ],
                axis=0,
            )
            span = slice(ms[0] * part, (ms[-1] + 1) * part)
            acc[r, span, :] += jnp.dot(
                lhs, table[q, l], preferred_element_type=jnp.float32
            )
        return carry

    lax.fori_loop(0, count[0], one_tile, 0)
    basis = [[], [], [], []]
    for b in range(blocks):
        d = [acc[b, m * part : (m + 1) * part, :] for m in range(9)]
        values = (
            d[0],
            d[0] * d[0],
            d[1] * d[1] + d[2] * d[2] + d[3] * d[3],
            d[4] * d[4] + d[5] * d[5] + d[6] * d[6] + d[7] * d[7] + d[8] * d[8],
        )
        for kept, value in zip(basis, values):
            kept.append(value.astype(jnp.bfloat16))
    mixed = None
    for q in range(4):
        term = jnp.dot(
            jnp.concatenate(basis[q], axis=0), mix[q], preferred_element_type=jnp.float32
        )
        mixed = term if mixed is None else mixed + term
    mixed = mixed / (1.0 + jnp.exp(-mixed))
    feat = jnp.concatenate([feat_rows[b, mine, :] for b in range(blocks)], axis=0)
    hidden = feat + mixed
    my_atom = (lax.broadcasted_iota(jnp.int32, (part, 1), 0) + h * part).astype(jnp.float32)
    present = jnp.concatenate(
        [(my_atom < place[3:4, b : b + 1]).astype(jnp.float32) for b in range(blocks)], axis=0
    )
    hidden = hidden * present
    upd[...] = hidden.T.astype(jnp.bfloat16)
    energy = jnp.sum((hidden * w[3 * basis_count : 3 * basis_count + 1, :]).T, axis=0, keepdims=True)
    square = jnp.sum(energy * energy, axis=1, keepdims=True)
    atoms = jnp.sum(present, axis=0, keepdims=True)
    stats[...] = jnp.zeros_like(stats)
    stats[0:1, :] = energy
    stats[1:2, :] = jnp.broadcast_to(square, energy.shape)
    stats[2:3, :] = jnp.broadcast_to(atoms, energy.shape)


def return_kernel(
    shape, blocks, upd, stats, updated, energies, scale_ref,
    rows_in, stats_in, group_sum, sums_in, sems_s, sems_r, sums_s, sums_r,
):
    groups, peers = shape
    g, h = lax.axis_index("atoms"), lax.axis_index("chan")
    chans = updated.shape[0]
    part = upd.shape[1] // blocks
    barrier = pltpu.get_barrier_semaphore()
    for d in range(1, peers):
        pl.semaphore_signal(
            barrier, inc=1, device_id=(g, lax.rem(h + d, peers)), device_id_type=MESH
        )

    def greet(d, carry):
        pl.semaphore_signal(
            barrier, inc=1, device_id=(lax.rem(g + d, groups), h), device_id_type=MESH
        )
        return carry

    lax.fori_loop(1, groups, greet, 0)
    pl.semaphore_wait(barrier, peers + groups - 2)
    copies = []

    def send(src, dst, device):
        slot = len(copies)
        copy = pltpu.make_async_remote_copy(
            src_ref=src,
            dst_ref=dst,
            send_sem=sems_s.at[slot],
            recv_sem=sems_r.at[slot],
            device_id=device,
            device_id_type=MESH,
        )
        copy.start()
        copies.append(copy)

    for d in range(1, peers):
        send(stats, stats_in.at[h], (g, lax.rem(h + d, peers)))
    for d in range(1, peers):
        to = lax.rem(h + d, peers)
        send(
            upd.at[pl.ds(pl.multiple_of(to * chans, chans), chans), :],
            rows_in.at[h],
            (g, to),
        )
    stats_in[h] = stats[...]
    rows_in[h] = upd[pl.ds(pl.multiple_of(h * chans, chans), chans), :]
    for copy in copies[: peers - 1]:
        copy.wait()
    total = stats_in[0]
    for n in range(1, peers):
        total = total + stats_in[n]
    group_sum[...] = jnp.broadcast_to(total[:, 0:1], group_sum.shape)

    def sum_copy(d):
        return pltpu.make_async_remote_copy(
            src_ref=group_sum,
            dst_ref=sums_in.at[d],
            send_sem=sums_s.at[d],
            recv_sem=sums_r.at[d],
            device_id=(lax.rem(g + d, groups), h),
            device_id_type=MESH,
        )

    def start(d, carry):
        sum_copy(d).start()
        return carry

    lax.fori_loop(1, groups, start, 0)
    for copy in copies[peers - 1 :]:
        copy.wait()
    pieces = [rows_in[n].astype(jnp.float32) for n in range(peers)]
    for b in range(blocks):
        span = slice(b * part, (b + 1) * part)
        updated[:, b * part * peers : (b + 1) * part * peers] = jnp.concatenate(
            [piece[:, span] for piece in pieces], axis=1
        ).astype(jnp.bfloat16)
    energy = jnp.concatenate(
        [
            stats_in[n][:, b * part : (b + 1) * part]
            for b in range(blocks)
            for n in range(peers)
        ],
        axis=1,
    )[0:1, :]

    def finish(d, whole):
        sum_copy(d).wait()
        return whole + sums_in[d]

    whole = lax.fori_loop(1, groups, finish, group_sum[...])
    scale = jnp.sqrt(1.0 + whole[1:2, :] / whole[2:3, :])
    energies[...] = energy / scale[:, 0:1]
    scale_ref[...] = scale


def per_device(
    shape, features, positions, block_counts, radial_w, mix_w, read_w, ghost_lists, tile_pairs,
    tile_count,
):
    groups, peers = shape
    chans, atoms = features.shape
    blocks = block_counts.shape[0]
    width = atoms // blocks
    basis_count = radial_w.shape[0]
    channels = mix_w.shape[1]
    part = width // peers
    f32 = jnp.float32
    extra = jnp.concatenate([block_counts, ghost_lists.reshape(-1)]).astype(f32)
    place = jnp.concatenate(
        [positions, jnp.pad(extra, (0, atoms - extra.shape[0]))[None], jnp.zeros((4, atoms), f32)]
    )
    weights = jnp.concatenate(
        [radial_w.reshape(-1, chans), read_w[None], jnp.zeros((7, chans), f32)]
    )
    vmem = pl.BlockSpec(memory_space=pltpu.VMEM)
    smem = pl.BlockSpec(memory_space=pltpu.SMEM)
    dma = pltpu.SemaphoreType.DMA
    first = 2 * peers * (blocks // 2) + 2 + 2 * (peers - 1)
    feats, places, walls = pl.pallas_call(
        functools.partial(gather_kernel, shape, blocks),
        out_shape=(
            jax.ShapeDtypeStruct((channels, 2 * atoms), jnp.bfloat16),
            jax.ShapeDtypeStruct((2,) + place.shape, f32),
            jax.ShapeDtypeStruct((peers,) + weights.shape, f32),
        ),
        in_specs=[vmem] * 3,
        out_specs=(vmem,) * 3,
        scratch_shapes=[dma((first,)), dma((first,)), dma((2,))],
        compiler_params=pltpu.CompilerParams(collective_id=0, has_side_effects=True),
        name="gather",
    )(features, place, weights)
    upd, stats = pl.pallas_call(
        functools.partial(compute_kernel, peers, blocks, basis_count),
        out_shape=(
            jax.ShapeDtypeStruct((channels, blocks * part), jnp.bfloat16),
            jax.ShapeDtypeStruct((8, blocks * part), f32),
        ),
        in_specs=[smem, smem] + [vmem] * 5,
        out_specs=(vmem, vmem),
        scratch_shapes=[
            pltpu.VMEM((2 * blocks, 3, basis_count * width, channels), jnp.bfloat16),
            pltpu.VMEM((2 * blocks, 8, width), f32),
            pltpu.VMEM((3 * blocks, width, width), f32),
            pltpu.VMEM((blocks, width, channels), f32),
            pltpu.VMEM((blocks, 9 * part, channels), f32),
        ],
        compiler_params=pltpu.CompilerParams(vmem_limit_bytes=50 * 1024 * 1024),
        name="compute",
    )(tile_pairs, tile_count, feats, place, places, walls, mix_w)
    last = 2 * (peers - 1)
    updated, energies, scale = pl.pallas_call(
        functools.partial(return_kernel, shape, blocks),
        out_shape=(
            jax.ShapeDtypeStruct((chans, atoms), jnp.bfloat16),
            jax.ShapeDtypeStruct((1, atoms), f32),
            jax.ShapeDtypeStruct((1, 128), f32),
        ),
        in_specs=[vmem] * 2,
        out_specs=(vmem,) * 3,
        scratch_shapes=[
            pltpu.VMEM((peers, chans, blocks * part), jnp.bfloat16),
            pltpu.VMEM((peers, 8, blocks * part), f32),
            pltpu.VMEM((8, 128), f32),
            pltpu.VMEM((groups, 8, 128), f32),
            dma((last,)),
            dma((last,)),
            dma((groups,)),
            dma((groups,)),
        ],
        compiler_params=pltpu.CompilerParams(collective_id=1, has_side_effects=True),
        name="hand_back",
    )(upd, stats)
    return updated, energies.reshape(-1), scale[0, 0]


def solution(mesh):
    shape = (mesh.shape["atoms"], mesh.shape["chan"])
    in_specs = (
        P("chan", "atoms"),
        P(None, "atoms"),
        P("atoms"),
        P(None, None, "chan"),
        P(),
        P("chan"),
        P("atoms", None, None),
        P("atoms", None, None),
        P("atoms"),
    )
    out_specs = (P("chan", "atoms"), P("atoms"), P())
    return jax.shard_map(
        functools.partial(per_device, shape),
        mesh=mesh,
        in_specs=in_specs,
        out_specs=out_specs,
        check_vma=False,
    )
```

time: 307 us -> 51.6 us (0.17)
  matrix products: 129 us -> 0 us
  blocking collectives: 82.6 us -> 0 us
  Pallas kernels: 0 us -> 36.5 us
  local copies, waits for them, and re-layouts: 40.1 us -> 8.16 us
  other arithmetic: 34.7 us -> 3.42 us
  starting transfers between devices: 12 us -> 0 us
    dot_general x12 -> x0, matrix products: 129 us -> none  [the longest x5 92.3 us: tile_term(): jnp.einsum('kmc,ckmi->cmi', table, partial_sums, precision=lax.Precision....]
    psum x2 -> x0, blocking collectives: 80.4 us -> none  [the longest x1 77.9 us: per_device(): lax.psum((jnp.sum(present_flat * energy * energy), jnp.sum(present_flat))...]
    pallas_call x0 -> x3, Pallas kernels: none -> 36.5 us  [the longest x1 12.7 us: per_device(): pl.pallas_call(functools.partial(compute_kernel, peers, blocks, basis_cou...]
    gather x31 -> x0, local copies, waits for them, and re-layouts: 29.7 us -> none  [the longest x5 6.62 us: one_turn(): codes = tile_list[tile_ids, 1]]
    ppermute x4 -> x0, starting transfers between devices: 12 us -> none  [the longest x2 9.41 us: extended(): lax.ppermute(lax.slice_in_dim(block, block.shape[dim] - width, None, axis...]
    exp x5 -> x0, other arithmetic: 8.63 us -> none  [tile_kernel(): jnp.exp(-radial_sharp * jnp.square(distance[None] - centers[:, None, None]))]
    unnamed x8 -> x22, local copies, waits for them, and re-layouts: 0.03 us -> 7.23 us
    scatter-add x5 -> x0, other arithmetic: 6.87 us -> none  [one_turn(): return totals.at[receivers].add(terms * weights[:, None, None, None])]
  transfers between devices with their start and end apart: 4 -> 0, of which waited for: 1 -> 0; matrix products, arithmetic and copies ran while one was open for 2% -> 0% of each run, Pallas kernels for 0% -> 0%
where the time goes in v1:
time: 51.6 us; the launch traced here: 50.7 us
  Pallas kernels  36.5 us (71%)
  local copies, waits for them, and re-layouts  8.16 us (16%)
  other arithmetic  3.42 us (7%)
  between operations  2.55 us (5%)
    pallas_call x1, Pallas kernels, per_device(): pl.pallas_call(functools.partial(compute_kernel, peers, blocks, basis_cou...  12.7 us
    pallas_call x1, Pallas kernels, per_device(): pl.pallas_call(functools.partial(gather_kernel, shape, blocks), out_shape...  12.1 us
    pallas_call x1, Pallas kernels, per_device(): pl.pallas_call(functools.partial(return_kernel, shape, blocks), out_shape...  11.8 us
    unnamed x22, local copies, waits for them, and re-layouts  7.23 us
    concatenate x1, other arithmetic, per_device(): jnp.concatenate([positions, jnp.pad(extra, (0, atoms - extra.shape[0]))[N...  1.37 us
    concatenate x1, other arithmetic, per_device(): jnp.concatenate([radial_w.reshape(-1, chans), read_w[None], jnp.zeros((7,...  1.32 us

profile of v1, /device:TPU:0, one launch (start us, length us, event | category | flops | bytes accessed | tf_op | source)
XLA Modules:
  0.0 50.7 jit_solution(10187379833985992386)
XLA Ops:
  0.6 0.0 copy-start.2
  1.3 0.8 %reshape.15 = s32[4]{0:T(128)S(1)} reshape(s32[1,2,2]{2,1,0:T(2,128)} %param.15) | data formatting | bytes 32 | tf_op jit(solution)/shard_map/reshape | solution.py:340
  2.1 0.7 %add_convert_fusion = f32[8]{0:T(128)S(1)} fusion(s32[4]{0:T(128)S(1)} %reshape.15, s32[4]{0:T(128)} %param.11), kind=kLoop, calls=%fused_computation.2 | loop fusion | flops 16 | bytes 64 | tf_op jit(solution)/shard_map/convert_element_type | solution.py:340
  2.8 0.1 pad.7.clone
  2.9 0.1 pad.10.clone
  3.0 0.8 %copy.15.pairs = s32[1,24,2]{2,1,0:T(8,128)S(1)} copy(s32[1,24,2]{1,2,0:T(2,128)} %param.16) | data formatting | bytes 384 | tf_op args[7]
  3.7 1.4 %maximum_maximum_fusion.place_ref.place = f32[8,512]{1,0:T(8,128)} fusion(f32[1,512]{1,0:T(1,128)S(1)} %bitcast.5, f32[3,512]{1,0:T(4,128)} %param.10, f32[8]{0:T(128)S(1)} %pad.10.clone), kind=kLoop, calls=%fused_computation | loop fusion | flops 8192 | bytes 24608 | tf_op jit(solution)/shard_map/concatenate | solution.py:341
  5.1 0.7 %copy.14 = f32[8,3,64]{2,1,0:T(4,128)S(1)} copy(f32[8,3,64]{2,0,1:T(8,128)} %param.12) | data formatting | bytes 12288 | tf_op args[3]
  5.8 1.3 %maximum_maximum_fusion.1.w_ref = f32[32,64]{1,0:T(8,128)} fusion(f32[1,64]{1,0:T(1,128)} %bitcast.7, f32[24,64]{1,0:T(8,128)S(1)} %reshape.16, f32[32]{0:T(128)S(1)} %pad.7.clone), kind=kLoop, calls=%fused_computation.1 | loop fusion | flops 4096 | bytes 14720 | tf_op jit(solution)/shard_map/concatenate | solution.py:344
  7.2 0.0 copy-start.1
  7.2 12.1 %gather.1 = (bf16[128,1024]{1,0:T(8,128)(2,1)}, f32[2,8,512]{2,1,0:T(8,128)}, f32[2,32,64]{2,1,0:T(8,128)}) custom-call(bf16[64,512]{1,0:T(8,128)(2,1)} %feat_ref.1, f32[8,512]{1,0:T(8,128)} %maximum_maximum_fusion.place_ref.place, f32[32,64]{1,0:T(8,128)} %maximum_maximum_fusion.1.w_ref), custom_call_target="tpu_custom_call" | custom-call | tf_op jit(solution)/shard_map/gather/pallas_call | solution.py:351
  19.2 0.0 copy-done.2
  19.2 0.0 copy-done.1
  19.2 0.0 copy-start
  19.3 0.9 %copy-done = bf16[128,1024]{1,0:T(8,128)(2,1)S(1)} copy-done((bf16[128,1024]{1,0:T(8,128)(2,1)S(1)}, bf16[128,1024]{1,0:T(8,128)(2,1)}, u32[]{:S(2)}) %copy-start) | copy-done | bytes 262168
  20.2 0.0 copy-start.4
  20.2 0.8 %copy-done.4 = f32[2,8,512]{2,1,0:T(8,128)S(1)} copy-done((f32[2,8,512]{2,1,0:T(8,128)S(1)}, f32[2,8,512]{2,1,0:T(8,128)}, u32[]{:S(2)}) %copy-start.4) | copy-done | bytes 32792
  21.0 0.0 copy-start.5
  21.0 0.8 %copy-done.5 = f32[2,32,64]{2,1,0:T(8,128)S(1)} copy-done((f32[2,32,64]{2,1,0:T(8,128)S(1)}, f32[2,32,64]{2,1,0:T(8,128)}, u32[]{:S(2)}) %copy-start.5) | copy-done | bytes 16408
  21.7 12.7 %compute.1 = (bf16[128,256]{1,0:T(8,128)(2,1)S(1)}, f32[8,256]{1,0:T(8,128)S(1)}) custom-call(s32[1,24,2]{2,1,0:T(8,128)S(1)} %copy.15.pairs, s32[1]{0:T(128)S(6)} %copy.19.count, bf16[128,1024]{1,0:T(8,128)(2,1)S(1)} %copy-done, f32[8,512]{1,0:T(8,128)S(1)} %copy-done.1, f32[2,8,512]{2,1,0:T(8,128)S(1)} %copy-done.4, f32[2,32,64]{2,1,0:T(8,128)S(1)} %copy-done.5, ...), custom_call_target="tpu_custom_call" | custom-call | tf_op jit(solution)/shard_map/compute/pallas_call | solution.py:364
  34.4 0.0 copy-start.3
  34.4 0.6 %copy-done.3 = bf16[128,256]{1,0:T(8,128)(2,1)} copy-done((bf16[128,256]{1,0:T(8,128)(2,1)}, bf16[128,256]{1,0:T(8,128)(2,1)S(1)}, u32[]{:S(2)}) %copy-start.3) | copy-done | bytes 65560
  35.0 0.0 copy-start.6
  35.0 0.6 %copy-done.6 = f32[8,256]{1,0:T(8,128)} copy-done((f32[8,256]{1,0:T(8,128)}, f32[8,256]{1,0:T(8,128)S(1)}, u32[]{:S(2)}) %copy-start.6) | copy-done | bytes 8216
  35.6 11.8 %hand_back.1 = (bf16[64,512]{1,0:T(8,128)(2,1)}, f32[1,512]{1,0:T(1,128)}, f32[1,128]{1,0:T(1,128)}) custom-call(bf16[128,256]{1,0:T(8,128)(2,1)} %copy-done.3, f32[8,256]{1,0:T(8,128)} %copy-done.6), custom_call_target="tpu_custom_call" | custom-call | tf_op jit(solution)/shard_map/hand_back/pallas_call | solution.py:383
  47.4 0.0 copy-start.7
  47.4 1.5 %copy.20 = bf16[64,512]{1,0:T(8,128)(2,1)} copy(bf16[64,512]{1,0:T(8,128)(2,1)} %get-tuple-element.22) | data formatting | bytes 131072
  48.9 0.0 copy-done.7
  48.9 0.0 copy-start.8
  48.9 0.6 %copy.21 = f32[512]{0:T(512)} copy(f32[512]{0:T(512)S(1)} %bitcast.6) | data formatting | bytes 4096
  49.5 0.0 copy-done.8
  (4 shorter events, 0.0 us)
Async XLA Ops:
  0.6 18.6 %copy-start.2 = (bf16[4,128,128]{2,1,0:T(8,128)(2,1)S(1)}, bf16[4,128,128]{2,1,0:T(8,128)(2,1)}, u32[]{:S(2)}) copy-start(bf16[4,128,128]{2,1,0:T(8,128)(2,1)} %mix.1) | copy-start | bytes 393220
  7.2 12.1 %copy-start.1 = (f32[8,512]{1,0:T(8,128)S(1)}, f32[8,512]{1,0:T(8,128)}, u32[]{:S(2)}) copy-start(f32[8,512]{1,0:T(8,128)} %maximum_maximum_fusion.place_ref.place) | copy-start | bytes 49156
  19.2 1.0 %copy-start = (bf16[128,1024]{1,0:T(8,128)(2,1)S(1)}, bf16[128,1024]{1,0:T(8,128)(2,1)}, u32[]{:S(2)}) copy-start(bf16[128,1024]{1,0:T(8,128)(2,1)} %get-tuple-element.11.feats) | copy-start | bytes 786436
  20.2 0.8 %copy-start.4 = (f32[2,8,512]{2,1,0:T(8,128)S(1)}, f32[2,8,512]{2,1,0:T(8,128)}, u32[]{:S(2)}) copy-start(f32[2,8,512]{2,1,0:T(8,128)} %get-tuple-element.12.places) | copy-start | bytes 98308
  21.0 0.8 %copy-start.5 = (f32[2,32,64]{2,1,0:T(8,128)S(1)}, f32[2,32,64]{2,1,0:T(8,128)}, u32[]{:S(2)}) copy-start(f32[2,32,64]{2,1,0:T(8,128)} %get-tuple-element.13.walls) | copy-start | bytes 49156
  34.4 0.6 %copy-start.3 = (bf16[128,256]{1,0:T(8,128)(2,1)}, bf16[128,256]{1,0:T(8,128)(2,1)S(1)}, u32[]{:S(2)}) copy-start(bf16[128,256]{1,0:T(8,128)(2,1)S(1)} %get-tuple-element.14.upd) | copy-start | bytes 196612
  35.0 0.6 %copy-start.6 = (f32[8,256]{1,0:T(8,128)}, f32[8,256]{1,0:T(8,128)S(1)}, u32[]{:S(2)}) copy-start(f32[8,256]{1,0:T(8,128)S(1)} %get-tuple-element.15.stats) | copy-start | bytes 24580
  47.4 1.5 %copy-start.7 = (f32[1,512]{1,0:T(1,128)S(1)}, f32[1,512]{1,0:T(1,128)}, u32[]{:S(2)}) copy-start(f32[1,512]{1,0:T(1,128)} %get-tuple-element.17) | copy-start | bytes 6148
  48.9 0.6 %copy-start.8 = (f32[1,128]{1,0:T(1,128)S(1)}, f32[1,128]{1,0:T(1,128)}, u32[]{:S(2)}) copy-start(f32[1,128]{1,0:T(1,128)} %get-tuple-element.18) | copy-start | bytes 1540

commit v2 on v1

v2 whole, which is shorter than its diff:
```python
import functools

import jax
import jax.numpy as jnp
from jax import lax
from jax.experimental import pallas as pl
from jax.experimental.pallas import tpu as pltpu
from jax.sharding import PartitionSpec as P

root_three = 3.0**0.5
root_fifteen = 15.0**0.5
half_root_five = 0.5 * 5.0**0.5
half_root_fifteen = 0.5 * 15.0**0.5
cutoff_square = 9.0
soften = 0.25
center_step = 3.0 / 7.0
radial_sharp = 2.0
degrees = ((0,), (1, 2, 3), (4, 5, 6, 7, 8))
MESH = pl.DeviceIdType.MESH


def layer_kernel(
    shape, basis_count, pairs, count, feat_ref, where_ref, present_ref, list_ref, radial_ref,
    read_ref, mix, updated, energies, scale_ref,
    own_in, ghost_in, where_in, present_in, list_in, radial_in, read_in,
    table, spos, rpos, feat_rows, terms, upd, stats, rows_in, stats_in, group_sum, sums_in,
    local_sems, near_s, near_r, far_s, far_r, last_s, last_r, sums_s, sums_r,
):
    groups, peers = shape
    g, h = lax.axis_index("atoms"), lax.axis_index("chan")
    chans = feat_ref.shape[0]
    blocks = present_ref.shape[1]
    half = list_ref.shape[1]
    width = feat_ref.shape[1] // blocks
    tiles = pairs.shape[1]
    part = width // peers
    after, before = lax.rem(g + 1, groups), lax.rem(g + groups - 1, groups)
    barrier = pltpu.get_barrier_semaphore()

    def signal(device):
        pl.semaphore_signal(barrier, inc=1, device_id=device, device_id_type=MESH)

    for d in range(1, peers):
        to = lax.rem(h + d, peers)
        signal((g, to))
        signal((after, to))
        signal((before, to))

    def greet(d, carry):
        signal((lax.rem(g + d, groups), h))
        return carry

    lax.fori_loop(1, groups, greet, 0)
    locals_ = [
        pltpu.make_async_copy(feat_ref, own_in.at[h], local_sems.at[0]),
        pltpu.make_async_copy(radial_ref, radial_in.at[h], local_sems.at[1]),
        pltpu.make_async_copy(read_ref, read_in.at[h], local_sems.at[2]),
    ]
    for copy in locals_:
        copy.start()
    pl.semaphore_wait(barrier, 3 * (peers - 1) + groups - 1)

    def send(copies, sems, src, dst, device):
        slot = len(copies)
        copy = pltpu.make_async_remote_copy(
            src_ref=src,
            dst_ref=dst,
            send_sem=sems[0].at[slot],
            recv_sem=sems[1].at[slot],
            device_id=device,
            device_id_type=MESH,
        )
        copy.start()
        copies.append(copy)

    near, far, last = [], [], []
    for d in range(1, peers):
        to = (g, lax.rem(h + d, peers))
        send(near, (near_s, near_r), feat_ref, own_in.at[h], to)
        send(near, (near_s, near_r), radial_ref, radial_in.at[h], to)
        send(near, (near_s, near_r), read_ref, read_in.at[h], to)
    for d in range(peers):
        to = lax.rem(h + d, peers)
        for n in range(half):
            for side, there in ((0, after), (1, before)):
                block = 2 * n + 1 - side
                send(
                    far,
                    (far_s, far_r),
                    feat_ref.at[:, pl.ds(block * width, width)],
                    ghost_in.at[side * half + n, h],
                    (there, to),
                )
    for side, there in ((0, after), (1, before)):
        send(far, (far_s, far_r), where_ref, where_in.at[side], (there, h))
        send(far, (far_s, far_r), present_ref, present_in.at[side], (there, h))
        send(far, (far_s, far_r), list_ref, list_in.at[side], (there, h))

    mine = pl.ds(pl.multiple_of(h * part, part), part)
    atom = lax.broadcasted_iota(jnp.int32, (width, 1), 0)
    for b in range(blocks):
        spos[b, 0:3, :] = where_ref[:, b * width : (b + 1) * width]
        for axis in range(3):
            rpos[3 * b + axis] = jnp.broadcast_to(
                where_ref[axis : axis + 1, b * width : (b + 1) * width], (width, width)
            ).T
    diagonal = (
        lax.broadcasted_iota(jnp.int32, (part, width), 0) + h * part
        == lax.broadcasted_iota(jnp.int32, (part, width), 1)
    ).astype(jnp.float32)
    terms[0] = jnp.zeros_like(terms[0])
    for copy in locals_:
        copy.wait()
    for copy in near:
        copy.wait()
    weights = [
        jnp.concatenate([radial_in[n, l] for n in range(peers)], axis=1) for l in range(3)
    ]
    read = jnp.concatenate([read_in[n] for n in range(peers)], axis=1)

    def store_source(code, rows, present):
        masked = jnp.where(atom < present, rows, 0.0)
        for l in range(3):
            for k in range(basis_count):
                table[code, l, k * width : (k + 1) * width, :] = (
                    masked * weights[l][k : k + 1, :]
                ).astype(jnp.bfloat16)

    for b in range(blocks):
        rows = jnp.concatenate(
            [own_in[n, :, b * width : (b + 1) * width] for n in range(peers)], axis=0
        ).astype(jnp.float32).T
        feat_rows[b] = rows
        store_source(b, rows, present_ref[0:1, b : b + 1])

    def one_tile(t, lasts):
        r, q = pairs[0, t], pairs[1, t]
        dx = spos[q, 0:1, :] - rpos[3 * r, mine, :]
        dy = spos[q, 1:2, :] - rpos[3 * r + 1, mine, :]
        dz = spos[q, 2:3, :] - rpos[3 * r + 2, mine, :]
        d2 = dx * dx + dy * dy + dz * dz
        is_self = (r == q).astype(jnp.float32)
        alive = (t < count[0]).astype(jnp.float32)
        edge = jnp.maximum(1.0 - d2 * (1.0 / cutoff_square), 0.0)
        cut = edge * edge * (alive - alive * is_self * diagonal)
        inverse = lax.rsqrt(d2 + soften)
        dist = (d2 + soften) * inverse
        x, y, z = dx * inverse, dy * inverse, dz * inverse
        cx, cy = cut * root_fifteen * x, cut * root_fifteen * y
        cut3 = cut * root_three
        angular = (
            cut,
            cut3 * x,
            cut3 * y,
            cut3 * z,
            cx * y,
            cy * z,
            cut * half_root_five * (2.0 * z * z - x * x - y * y),
            cx * z,
            cut * half_root_fifteen * (x * x - y * y),
        )
        radial = []
        for k in range(basis_count):
            off = dist - center_step * k
            radial.append(jnp.exp(-radial_sharp * off * off))
        previous = lasts[0]
        for b in range(1, blocks):
            previous = jnp.where(r == b, lasts[b], previous)
        for l, ms in enumerate(degrees):
            lhs = jnp.concatenate(
                [
                    jnp.concatenate(
                        [(radial[k] * angular[m]).astype(jnp.bfloat16) for k in range(basis_count)],
                        axis=1,
                    )
                    for m in ms
                ],
                axis=0,
            )
            span = slice(ms[0] * part, (ms[-1] + 1) * part)
            terms[t + 1, span, :] = terms[previous, span, :] + jnp.dot(
                lhs, table[q, l], preferred_element_type=jnp.float32
            )
        return tuple(jnp.where(r == b, t + 1, kept) for b, kept in enumerate(lasts))

    lasts = lax.fori_loop(0, blocks, one_tile, (jnp.int32(0),) * blocks)
    for copy in far:
        copy.wait()
    for side in range(2):
        for n in range(half):
            listed = list_in[side, 1 - side : 2 - side, n : n + 1]
            code = blocks + side * half + n
            rows, where, present = None, None, None
            for m in range(half):
                block = 2 * m + 1 - side
                new = (
                    jnp.concatenate(
                        [ghost_in[side * half + m, p] for p in range(peers)], axis=0
                    ).astype(jnp.float32),
                    where_in[side, :, block * width : (block + 1) * width],
                    present_in[side, 0:1, block : block + 1],
                )
                if m == 0:
                    rows, where, present = new
                else:
                    is_it = listed == block
                    rows = jnp.where(is_it, new[0], rows)
                    where = jnp.where(is_it, new[1], where)
                    present = jnp.where(is_it, new[2], present)
            store_source(code, rows.T, present)
            spos[code, 0:3, :] = where
    lasts = lax.fori_loop(blocks, tiles, one_tile, lasts)

    basis = [[], [], [], []]
    for b in range(blocks):
        d = [terms[lasts[b], m * part : (m + 1) * part, :] for m in range(9)]
        values = (
            d[0],
            d[0] * d[0],
            d[1] * d[1] + d[2] * d[2] + d[3] * d[3],
            d[4] * d[4] + d[5] * d[5] + d[6] * d[6] + d[7] * d[7] + d[8] * d[8],
        )
        for kept, value in zip(basis, values):
            kept.append(value.astype(jnp.bfloat16))
    mixed = None
    for q in range(4):
        term = jnp.dot(
            jnp.concatenate(basis[q], axis=0), mix[q], preferred_element_type=jnp.float32
        )
        mixed = term if mixed is None else mixed + term
    mixed = mixed / (1.0 + jnp.exp(-mixed))
    feat = jnp.concatenate([feat_rows[b, mine, :] for b in range(blocks)], axis=0)
    my_atom = lax.broadcasted_iota(jnp.int32, (part, 1), 0) + h * part
    present = jnp.concatenate(
        [(my_atom < present_ref[0:1, b : b + 1]).astype(jnp.float32) for b in range(blocks)],
        axis=0,
    )
    hidden = (feat + mixed) * present
    energy = jnp.sum((hidden * read).T, axis=0, keepdims=True)
    square = jnp.sum(energy * energy, axis=1, keepdims=True)
    atoms = jnp.sum(present, axis=0, keepdims=True)
    stats[...] = jnp.concatenate(
        [
            energy,
            jnp.broadcast_to(square, energy.shape),
            jnp.broadcast_to(atoms, energy.shape),
            jnp.zeros((5, energy.shape[1]), jnp.float32),
        ],
        axis=0,
    )
    upd[...] = hidden.T.astype(jnp.bfloat16)
    for d in range(1, peers):
        send(last, (last_s, last_r), stats, stats_in.at[h], (g, lax.rem(h + d, peers)))
    for d in range(1, peers):
        to = lax.rem(h + d, peers)
        send(
            last,
            (last_s, last_r),
            upd.at[pl.ds(pl.multiple_of(to * chans, chans), chans), :],
            rows_in.at[h],
            (g, to),
        )
    stats_in[h] = stats[...]
    rows_in[h] = upd[pl.ds(pl.multiple_of(h * chans, chans), chans), :]
    for copy in last[: peers - 1]:
        copy.wait()
    total = stats_in[0]
    for n in range(1, peers):
        total = total + stats_in[n]
    group_sum[...] = jnp.broadcast_to(total[:, 0:1], group_sum.shape)

    def sum_copy(d):
        return pltpu.make_async_remote_copy(
            src_ref=group_sum,
            dst_ref=sums_in.at[g],
            send_sem=sums_s.at[d],
            recv_sem=sums_r.at[d],
            device_id=(lax.rem(g + d, groups), h),
            device_id_type=MESH,
        )

    def start(d, carry):
        sum_copy(d).start()
        return carry

    lax.fori_loop(1, groups, start, 0)
    sums_in[g] = group_sum[...]
    for copy in last[peers - 1 :]:
        copy.wait()
    pieces = [rows_in[n].astype(jnp.float32) for n in range(peers)]
    for b in range(blocks):
        span = slice(b * part, (b + 1) * part)
        updated[:, b * part * peers : (b + 1) * part * peers] = jnp.concatenate(
            [piece[:, span] for piece in pieces], axis=1
        ).astype(jnp.bfloat16)
    energy = jnp.concatenate(
        [
            stats_in[n][:, b * part : (b + 1) * part]
            for b in range(blocks)
            for n in range(peers)
        ],
        axis=1,
    )[0:1, :]

    def finish(d, carry):
        sum_copy(d).wait()
        return carry

    lax.fori_loop(1, groups, finish, 0)
    whole = jnp.sum(sums_in[...], axis=0)
    scale = jnp.sqrt(1.0 + whole[1:2, :] / whole[2:3, :])
    energies[...] = energy / scale[:, 0:1]
    scale_ref[...] = scale


def per_device(
    shape, features, positions, block_counts, radial_w, mix_w, read_w, ghost_lists, tile_pairs,
    tile_count,
):
    groups, peers = shape
    chans, atoms = features.shape
    blocks = block_counts.shape[0]
    half = ghost_lists.shape[2]
    width = atoms // blocks
    basis_count = radial_w.shape[0]
    channels = mix_w.shape[1]
    tiles = tile_pairs.shape[1]
    part = width // peers
    f32, bf16, i32 = jnp.float32, jnp.bfloat16, jnp.int32
    vmem = pl.BlockSpec(memory_space=pltpu.VMEM)
    smem = pl.BlockSpec(memory_space=pltpu.SMEM)
    dma = pltpu.SemaphoreType.DMA
    near, far, last = 3 * (peers - 1), 2 * peers * half + 6, 2 * (peers - 1)
    updated, energies, scale = pl.pallas_call(
        functools.partial(layer_kernel, shape, basis_count),
        out_shape=(
            jax.ShapeDtypeStruct((chans, atoms), bf16),
            jax.ShapeDtypeStruct((1, atoms), f32),
            jax.ShapeDtypeStruct((1, 128), f32),
        ),
        in_specs=[smem] * 2 + [vmem] * 7,
        out_specs=(vmem,) * 3,
        scratch_shapes=[
            pltpu.VMEM((peers, chans, atoms), bf16),
            pltpu.VMEM((2 * half, peers, chans, width), bf16),
            pltpu.VMEM((2, 3, atoms), f32),
            pltpu.VMEM((2, 1, blocks), i32),
            pltpu.VMEM((2, 2, half), i32),
            pltpu.VMEM((peers, 3, basis_count, chans), f32),
            pltpu.VMEM((peers, 1, chans), f32),
            pltpu.VMEM((2 * blocks, 3, basis_count * width, channels), bf16),
            pltpu.VMEM((2 * blocks, 8, width), f32),
            pltpu.VMEM((3 * blocks, width, width), f32),
            pltpu.VMEM((blocks, width, channels), f32),
            pltpu.VMEM((tiles + 1, 9 * part, channels), f32),
            pltpu.VMEM((channels, blocks * part), bf16),
            pltpu.VMEM((8, blocks * part), f32),
            pltpu.VMEM((peers, chans, blocks * part), bf16),
            pltpu.VMEM((peers, 8, blocks * part), f32),
            pltpu.VMEM((8, 128), f32),
            pltpu.VMEM((groups, 8, 128), f32),
            dma((3,)),
            dma((near,)),
            dma((near,)),
            dma((far,)),
            dma((far,)),
            dma((last,)),
            dma((last,)),
            dma((groups,)),
            dma((groups,)),
        ],
        compiler_params=pltpu.CompilerParams(
            collective_id=0, has_side_effects=True, vmem_limit_bytes=50 * 1024 * 1024
        ),
        name="layer",
    )(
        tile_pairs[0].T,
        tile_count,
        features,
        positions,
        block_counts[None],
        ghost_lists[0],
        radial_w.transpose(1, 0, 2),
        read_w[None],
        mix_w,
    )
    return updated, energies.reshape(-1), scale[0, 0]


def solution(mesh):
    shape = (mesh.shape["atoms"], mesh.shape["chan"])
    in_specs = (
        P("chan", "atoms"),
        P(None, "atoms"),
        P("atoms"),
        P(None, None, "chan"),
        P(),
        P("chan"),
        P("atoms", None, None),
        P("atoms", None, None),
        P("atoms"),
    )
    out_specs = (P("chan", "atoms"), P("atoms"), P())
    return jax.shard_map(
        functools.partial(per_device, shape),
        mesh=mesh,
        in_specs=in_specs,
        out_specs=out_specs,
        check_vma=False,
    )
```

time: 51.6 us -> 38.3 us (0.74); the launches traced: 50.7 us -> 38 us
  Pallas kernels: 36.5 us -> 31.2 us
  local copies, waits for them, and re-layouts: 8.16 us -> 4.34 us
  other arithmetic: 3.42 us -> 0 us
    pallas_call x3 -> x1, Pallas kernels: 36.5 us -> 31.2 us  [per_device(): pl.pallas_call(functools.partial(layer_kernel, shape, basis_count), out_s...]
    unnamed x22 -> x18, local copies, waits for them, and re-layouts: 7.23 us -> 4.34 us
    concatenate x2 -> x0, other arithmetic: 2.69 us -> none  [the longest x1 1.37 us: per_device(): jnp.concatenate([positions, jnp.pad(extra, (0, atoms - extra.shape[0]))[N...]
    reshape x2 -> x0, local copies, waits for them, and re-layouts: 0.77 us -> none  [the longest x1 0.76 us: per_device(): extra = jnp.concatenate([block_counts, ghost_lists.reshape(-1)]).astype(f32)]
    convert_element_type x1 -> x0, other arithmetic: 0.73 us -> none  [per_device(): extra = jnp.concatenate([block_counts, ghost_lists.reshape(-1)]).astype(f32)]
where the time goes in v2:
time: 38.3 us; the launch traced here: 38 us
  Pallas kernels  31.2 us (81%)
  local copies, waits for them, and re-layouts  4.34 us (11%)
  between operations  2.52 us (7%)
    pallas_call x1, Pallas kernels, per_device(): pl.pallas_call(functools.partial(layer_kernel, shape, basis_count), out_s...  31.2 us
    unnamed x18, local copies, waits for them, and re-layouts  4.34 us

profile of v2, /device:TPU:0, one launch (start us, length us, event | category | flops | bytes accessed | tf_op | source)
XLA Modules:
  0.0 38.0 jit_solution(13284863019262436468)
XLA Ops:
  0.6 0.0 copy-start.3
  1.3 0.0 copy-start.5
  1.3 0.0 copy-start.7
  1.3 0.0 copy-start.4
  1.3 0.0 copy-start.6
  1.3 0.0 copy-done.3
  1.4 0.6 %copy-done.5 = s32[1,2,2]{2,1,0:T(2,128)S(1)} copy-done((s32[1,2,2]{2,1,0:T(2,128)S(1)}, s32[1,2,2]{2,1,0:T(2,128)}, u32[]{:S(2)}) %copy-start.5) | copy-done | bytes 40
  2.0 0.0 copy-done.7
  2.0 0.0 copy-done.4
  2.0 0.0 copy-done.6
  2.0 0.0 copy-start
  2.0 0.9 %copy-done = bf16[4,128,128]{2,1,0:T(8,128)(2,1)S(1)} copy-done((bf16[4,128,128]{2,1,0:T(8,128)(2,1)S(1)}, bf16[4,128,128]{2,1,0:T(8,128)(2,1)}, u32[]{:S(2)}) %copy-start) | copy-done | bytes 131096
  2.9 0.0 copy-start.1
  2.9 0.8 %copy-done.1 = bf16[64,512]{1,0:T(8,128)(2,1)S(1)} copy-done((bf16[64,512]{1,0:T(8,128)(2,1)S(1)}, bf16[64,512]{1,0:T(8,128)(2,1)}, u32[]{:S(2)}) %copy-start.1) | copy-done | bytes 65560
  3.8 0.0 copy-start.2
  3.8 0.7 %copy-done.2 = f32[8,3,64]{2,0,1:T(8,128)S(1)} copy-done((f32[8,3,64]{2,0,1:T(8,128)S(1)}, f32[8,3,64]{2,0,1:T(8,128)}, u32[]{:S(2)}) %copy-start.2) | copy-done | bytes 6168
  4.5 31.2 %layer.1 = (bf16[64,512]{1,0:T(8,128)(2,1)S(1)}, f32[1,512]{1,0:T(1,128)S(1)}, f32[1,128]{1,0:T(1,128)S(1)}) custom-call(s32[2,24]{1,0:T(2,128)S(1)} %bitcast.12, s32[1]{0:T(128)S(6)} %copy.15.count, bf16[64,512]{1,0:T(8,128)(2,1)S(1)} %copy-done.1, f32[3,512]{1,0:T(4,128)S(1)} %copy-done.3, s32[1,4]{1,0:T(1,128)S(1)} %bitcast.14, s32[2,2]{1,0:T(2,128)S(1)} %bitcast.13, ...), custom_call_target="tpu_custom_call" | custom-call | tf_op jit(solution)/shard_map/layer/pallas_call | solution.py:334
  35.6 0.6 %copy.16 = bf16[64,512]{1,0:T(8,128)(2,1)} copy(bf16[64,512]{1,0:T(8,128)(2,1)S(1)} %get-tuple-element.12) | data formatting | bytes 131072
  36.3 0.6 %copy.17 = f32[512]{0:T(512)} copy(f32[512]{0:T(512)S(1)} %bitcast.11) | data formatting | bytes 4096
Async XLA Ops:
  0.6 0.7 %copy-start.3 = (f32[3,512]{1,0:T(4,128)S(1)}, f32[3,512]{1,0:T(4,128)}, u32[]{:S(2)}) copy-start(f32[3,512]{1,0:T(4,128)} %where_ref.1) | copy-start | bytes 18436
  1.3 0.7 %copy-start.5 = (s32[1,2,2]{2,1,0:T(2,128)S(1)}, s32[1,2,2]{2,1,0:T(2,128)}, u32[]{:S(2)}) copy-start(s32[1,2,2]{2,1,0:T(2,128)} %param.15) | copy-start | bytes 52
  1.3 0.7 %copy-start.7 = (f32[64]{0:T(128)S(1)}, f32[64]{0:T(128)}, u32[]{:S(2)}) copy-start(f32[64]{0:T(128)} %param.14) | copy-start | bytes 772
  1.3 0.7 %copy-start.4 = (s32[1,24,2]{1,2,0:T(2,128)S(1)}, s32[1,24,2]{1,2,0:T(2,128)}, u32[]{:S(2)}) copy-start(s32[1,24,2]{1,2,0:T(2,128)} %param.16) | copy-start | bytes 580
  1.3 0.7 %copy-start.6 = (s32[4]{0:T(128)S(1)}, s32[4]{0:T(128)}, u32[]{:S(2)}) copy-start(s32[4]{0:T(128)} %param.11) | copy-start | bytes 52
  2.0 0.9 %copy-start = (bf16[4,128,128]{2,1,0:T(8,128)(2,1)S(1)}, bf16[4,128,128]{2,1,0:T(8,128)(2,1)}, u32[]{:S(2)}) copy-start(bf16[4,128,128]{2,1,0:T(8,128)(2,1)} %mix.1) | copy-start | bytes 393220
  2.9 0.8 %copy-start.1 = (bf16[64,512]{1,0:T(8,128)(2,1)S(1)}, bf16[64,512]{1,0:T(8,128)(2,1)}, u32[]{:S(2)}) copy-start(bf16[64,512]{1,0:T(8,128)(2,1)} %feat_ref.1) | copy-start | bytes 196612
  3.8 0.7 %copy-start.2 = (f32[8,3,64]{2,0,1:T(8,128)S(1)}, f32[8,3,64]{2,0,1:T(8,128)}, u32[]{:S(2)}) copy-start(f32[8,3,64]{2,0,1:T(8,128)} %param.12) | copy-start | bytes 18436

commit v3 on v2

--- a/solution.py
+++ b/solution.py
@@ -17,14 +17,15 @@
 radial_sharp = 2.0
 degrees = ((0,), (1, 2, 3), (4, 5, 6, 7, 8))
 MESH = pl.DeviceIdType.MESH
+UNROLL = 2
 
 
 def layer_kernel(
     shape, basis_count, pairs, count, feat_ref, where_ref, present_ref, list_ref, radial_ref,
-    read_ref, mix, updated, energies, scale_ref,
-    own_in, ghost_in, where_in, present_in, list_in, radial_in, read_in,
+    read_ref, mix_ref, updated, energies, scale_ref,
+    mix, own_in, ghost_in, where_in, present_in, list_in, radial_in, read_in,
     table, spos, rpos, feat_rows, terms, upd, stats, rows_in, stats_in, group_sum, sums_in,
-    local_sems, near_s, near_r, far_s, far_r, last_s, last_r, sums_s, sums_r,
+    local_sems, near_s, near_r, far_s, far_r, swap_s, swap_r, last_s, last_r, sums_s, sums_r,
 ):
     groups, peers = shape
     g, h = lax.axis_index("atoms"), lax.axis_index("chan")
@@ -43,8 +44,6 @@
     for d in range(1, peers):
         to = lax.rem(h + d, peers)
         signal((g, to))
-        signal((after, to))
-        signal((before, to))
 
     def greet(d, carry):
         signal((lax.rem(g + d, groups), h))
@@ -56,9 +55,11 @@
         pltpu.make_async_copy(radial_ref, radial_in.at[h], local_sems.at[1]),
         pltpu.make_async_copy(read_ref, read_in.at[h], local_sems.at[2]),
     ]
+    mix_copy = pltpu.make_async_copy(mix_ref, mix, local_sems.at[3])
     for copy in locals_:
         copy.start()
-    pl.semaphore_wait(barrier, 3 * (peers - 1) + groups - 1)
+    mix_copy.start()
+    pl.semaphore_wait(barrier, peers + groups - 2)
 
     def send(copies, sems, src, dst, device):
         slot = len(copies)
@@ -73,24 +74,22 @@
         copy.start()
         copies.append(copy)
 
-    near, far, last = [], [], []
+    near, far, swap, last = [], [], [], []
     for d in range(1, peers):
         to = (g, lax.rem(h + d, peers))
         send(near, (near_s, near_r), feat_ref, own_in.at[h], to)
         send(near, (near_s, near_r), radial_ref, radial_in.at[h], to)
         send(near, (near_s, near_r), read_ref, read_in.at[h], to)
-    for d in range(peers):
-        to = lax.rem(h + d, peers)
-        for n in range(half):
-            for side, there in ((0, after), (1, before)):
-                block = 2 * n + 1 - side
-                send(
-                    far,
-                    (far_s, far_r),
-                    feat_ref.at[:, pl.ds(block * width, width)],
-                    ghost_in.at[side * half + n, h],
-                    (there, to),
-                )
+    for n in range(half):
+        for side, there in ((0, after), (1, before)):
+            block = 2 * n + 1 - side
+            send(
+                far,
+                (far_s, far_r),
+                feat_ref.at[:, pl.ds(block * width, width)],
+                ghost_in.at[h, side * half + n],
+                (there, h),
+            )
     for side, there in ((0, after), (1, before)):
         send(far, (far_s, far_r), where_ref, where_in.at[side], (there, h))
         send(far, (far_s, far_r), present_ref, present_in.at[side], (there, h))
@@ -183,8 +182,14 @@
             )
         return tuple(jnp.where(r == b, t + 1, kept) for b, kept in enumerate(lasts))
 
-    lasts = lax.fori_loop(0, blocks, one_tile, (jnp.int32(0),) * blocks)
+    early = blocks // 2
+    lasts = lax.fori_loop(0, early, one_tile, (jnp.int32(0),) * blocks, unroll=UNROLL)
     for copy in far:
+        copy.wait()
+    for d in range(1, peers):
+        send(swap, (swap_s, swap_r), ghost_in.at[h], ghost_in.at[h], (g, lax.rem(h + d, peers)))
+    lasts = lax.fori_loop(early, blocks, one_tile, lasts, unroll=UNROLL)
+    for copy in swap:
         copy.wait()
     for side in range(2):
         for n in range(half):
@@ -195,7 +200,7 @@
                 block = 2 * m + 1 - side
                 new = (
                     jnp.concatenate(
-                        [ghost_in[side * half + m, p] for p in range(peers)], axis=0
+                        [ghost_in[p, side * half + m] for p in range(peers)], axis=0
                     ).astype(jnp.float32),
                     where_in[side, :, block * width : (block + 1) * width],
                     present_in[side, 0:1, block : block + 1],
@@ -209,7 +214,8 @@
                     present = jnp.where(is_it, new[2], present)
             store_source(code, rows.T, present)
             spos[code, 0:3, :] = where
-    lasts = lax.fori_loop(blocks, tiles, one_tile, lasts)
+    lasts = lax.fori_loop(blocks, tiles, one_tile, lasts, unroll=UNROLL)
+    mix_copy.wait()
 
     basis = [[], [], [], []]
     for b in range(blocks):
@@ -329,8 +335,9 @@
     f32, bf16, i32 = jnp.float32, jnp.bfloat16, jnp.int32
     vmem = pl.BlockSpec(memory_space=pltpu.VMEM)
     smem = pl.BlockSpec(memory_space=pltpu.SMEM)
+    hbm = pl.BlockSpec(memory_space=pltpu.HBM)
     dma = pltpu.SemaphoreType.DMA
-    near, far, last = 3 * (peers - 1), 2 * peers * half + 6, 2 * (peers - 1)
+    near, far, last = 3 * (peers - 1), 2 * half + 6, 2 * (peers - 1)
     updated, energies, scale = pl.pallas_call(
         functools.partial(layer_kernel, shape, basis_count),
         out_shape=(
@@ -338,11 +345,12 @@
             jax.ShapeDtypeStruct((1, atoms), f32),
             jax.ShapeDtypeStruct((1, 128), f32),
         ),
-        in_specs=[smem] * 2 + [vmem] * 7,
+        in_specs=[smem] * 2 + [hbm] + [vmem] * 3 + [hbm, vmem, hbm],
         out_specs=(vmem,) * 3,
         scratch_shapes=[
+            pltpu.VMEM(mix_w.shape, bf16),
             pltpu.VMEM((peers, chans, atoms), bf16),
-            pltpu.VMEM((2 * half, peers, chans, width), bf16),
+            pltpu.VMEM((peers, 2 * half, chans, width), bf16),
             pltpu.VMEM((2, 3, atoms), f32),
             pltpu.VMEM((2, 1, blocks), i32),
             pltpu.VMEM((2, 2, half), i32),
@@ -359,11 +367,13 @@
             pltpu.VMEM((peers, 8, blocks * part), f32),
             pltpu.VMEM((8, 128), f32),
             pltpu.VMEM((groups, 8, 128), f32),
-            dma((3,)),
+            dma((4,)),
             dma((near,)),
             dma((near,)),
             dma((far,)),
             dma((far,)),
+            dma((peers - 1,)),
+            dma((peers - 1,)),
             dma((last,)),
             dma((last,)),
             dma((groups,)),

time: 38.3 us -> 37.3 us (0.974)
  Pallas kernels: 31.2 us -> 30.2 us
    pallas_call x1, Pallas kernels: 31.2 us -> 30.2 us  [per_device(): pl.pallas_call(functools.partial(layer_kernel, shape, basis_count), out_s...]
where the time goes in v3:
time: 37.3 us; the launch traced here: 37 us
  Pallas kernels  30.2 us (81%)
  local copies, waits for them, and re-layouts  4.34 us (12%)
  between operations  2.52 us (7%)
    pallas_call x1, Pallas kernels, per_device(): pl.pallas_call(functools.partial(layer_kernel, shape, basis_count), out_s...  30.2 us
    unnamed x18, local copies, waits for them, and re-layouts  4.34 us

profile of v3, /device:TPU:0, one launch (start us, length us, event | category | flops | bytes accessed | tf_op | source)
XLA Modules:
  0.0 37.0 jit_solution(9991720030887928608)
XLA Ops:
  0.6 0.0 copy-start.3
  1.3 0.0 copy-start.5
  1.3 0.0 copy-start.7
  1.3 0.0 copy-start.4
  1.3 0.0 copy-start.6
  1.3 0.0 copy-done.3
  1.4 0.6 %copy-done.5 = s32[1,2,2]{2,1,0:T(2,128)S(1)} copy-done((s32[1,2,2]{2,1,0:T(2,128)S(1)}, s32[1,2,2]{2,1,0:T(2,128)}, u32[]{:S(2)}) %copy-start.5) | copy-done | bytes 40
  2.0 0.0 copy-done.7
  2.0 0.0 copy-done.4
  2.0 0.0 copy-done.6
  2.0 0.0 copy-start
  2.0 0.9 %copy-done = bf16[4,128,128]{2,1,0:T(8,128)(2,1)S(1)} copy-done((bf16[4,128,128]{2,1,0:T(8,128)(2,1)S(1)}, bf16[4,128,128]{2,1,0:T(8,128)(2,1)}, u32[]{:S(2)}) %copy-start) | copy-done | bytes 131096
  2.9 0.0 copy-start.1
  2.9 0.8 %copy-done.1 = bf16[64,512]{1,0:T(8,128)(2,1)S(1)} copy-done((bf16[64,512]{1,0:T(8,128)(2,1)S(1)}, bf16[64,512]{1,0:T(8,128)(2,1)}, u32[]{:S(2)}) %copy-start.1) | copy-done | bytes 65560
  3.8 0.0 copy-start.2
  3.8 0.7 %copy-done.2 = f32[8,3,64]{2,0,1:T(8,128)S(1)} copy-done((f32[8,3,64]{2,0,1:T(8,128)S(1)}, f32[8,3,64]{2,0,1:T(8,128)}, u32[]{:S(2)}) %copy-start.2) | copy-done | bytes 6168
  4.5 30.2 %layer.1 = (bf16[64,512]{1,0:T(8,128)(2,1)S(1)}, f32[1,512]{1,0:T(1,128)S(1)}, f32[1,128]{1,0:T(1,128)S(1)}) custom-call(s32[2,24]{1,0:T(2,128)S(1)} %bitcast.12, s32[1]{0:T(128)S(6)} %copy.15.count, bf16[64,512]{1,0:T(8,128)(2,1)S(1)} %copy-done.1, f32[3,512]{1,0:T(4,128)S(1)} %copy-done.3, s32[1,4]{1,0:T(1,128)S(1)} %bitcast.14, s32[2,2]{1,0:T(2,128)S(1)} %bitcast.13, ...), custom_call_target="tpu_custom_call" | custom-call | tf_op jit(solution)/shard_map/layer/pallas_call | solution.py:341
  34.6 0.6 %copy.16 = bf16[64,512]{1,0:T(8,128)(2,1)} copy(bf16[64,512]{1,0:T(8,128)(2,1)S(1)} %get-tuple-element.12) | data formatting | bytes 131072
  35.3 0.6 %copy.17 = f32[512]{0:T(512)} copy(f32[512]{0:T(512)S(1)} %bitcast.11) | data formatting | bytes 4096
Async XLA Ops:
  0.6 0.7 %copy-start.3 = (f32[3,512]{1,0:T(4,128)S(1)}, f32[3,512]{1,0:T(4,128)}, u32[]{:S(2)}) copy-start(f32[3,512]{1,0:T(4,128)} %where_ref.1) | copy-start | bytes 18436
  1.3 0.7 %copy-start.5 = (s32[1,2,2]{2,1,0:T(2,128)S(1)}, s32[1,2,2]{2,1,0:T(2,128)}, u32[]{:S(2)}) copy-start(s32[1,2,2]{2,1,0:T(2,128)} %param.15) | copy-start | bytes 52
  1.3 0.7 %copy-start.7 = (f32[64]{0:T(128)S(1)}, f32[64]{0:T(128)}, u32[]{:S(2)}) copy-start(f32[64]{0:T(128)} %param.14) | copy-start | bytes 772
  1.3 0.7 %copy-start.4 = (s32[1,24,2]{1,2,0:T(2,128)S(1)}, s32[1,24,2]{1,2,0:T(2,128)}, u32[]{:S(2)}) copy-start(s32[1,24,2]{1,2,0:T(2,128)} %param.16) | copy-start | bytes 580
  1.3 0.7 %copy-start.6 = (s32[4]{0:T(128)S(1)}, s32[4]{0:T(128)}, u32[]{:S(2)}) copy-start(s32[4]{0:T(128)} %param.11) | copy-start | bytes 52
  2.0 0.9 %copy-start = (bf16[4,128,128]{2,1,0:T(8,128)(2,1)S(1)}, bf16[4,128,128]{2,1,0:T(8,128)(2,1)}, u32[]{:S(2)}) copy-start(bf16[4,128,128]{2,1,0:T(8,128)(2,1)} %mix_ref.1) | copy-start | bytes 393220
  2.9 0.8 %copy-start.1 = (bf16[64,512]{1,0:T(8,128)(2,1)S(1)}, bf16[64,512]{1,0:T(8,128)(2,1)}, u32[]{:S(2)}) copy-start(bf16[64,512]{1,0:T(8,128)(2,1)} %feat_ref.1) | copy-start | bytes 196612
  3.8 0.7 %copy-start.2 = (f32[8,3,64]{2,0,1:T(8,128)S(1)}, f32[8,3,64]{2,0,1:T(8,128)}, u32[]{:S(2)}) copy-start(f32[8,3,64]{2,0,1:T(8,128)} %param.12) | copy-start | bytes 18436

commit v4 on v3

--- a/solution.py
+++ b/solution.py
@@ -21,9 +21,9 @@
 
 
 def layer_kernel(
-    shape, basis_count, pairs, count, feat_ref, where_ref, present_ref, list_ref, radial_ref,
+    shape, basis_count, pairs_ref, count_ref, feat_ref, where_hbm, present_hbm, list_ref, radial_ref,
     read_ref, mix_ref, updated, energies, scale_ref,
-    mix, own_in, ghost_in, where_in, present_in, list_in, radial_in, read_in,
+    pairs, count, where_ref, present_ref, mix, own_in, ghost_in, where_in, present_in, list_in, radial_in, read_in,
     table, spos, rpos, feat_rows, terms, upd, stats, rows_in, stats_in, group_sum, sums_in,
     local_sems, near_s, near_r, far_s, far_r, swap_s, swap_r, last_s, last_r, sums_s, sums_r,
 ):
@@ -59,6 +59,14 @@
     for copy in locals_:
         copy.start()
     mix_copy.start()
+    small = [
+        pltpu.make_async_copy(where_hbm, where_ref, local_sems.at[4]),
+        pltpu.make_async_copy(present_hbm, present_ref, local_sems.at[5]),
+        pltpu.make_async_copy(pairs_ref, pairs, local_sems.at[6]),
+        pltpu.make_async_copy(count_ref, count, local_sems.at[7]),
+    ]
+    for copy in small:
+        copy.start()
     pl.semaphore_wait(barrier, peers + groups - 2)
 
     def send(copies, sems, src, dst, device):
@@ -91,10 +99,12 @@
                 (there, h),
             )
     for side, there in ((0, after), (1, before)):
-        send(far, (far_s, far_r), where_ref, where_in.at[side], (there, h))
-        send(far, (far_s, far_r), present_ref, present_in.at[side], (there, h))
+        send(far, (far_s, far_r), where_hbm, where_in.at[side], (there, h))
+        send(far, (far_s, far_r), present_hbm, present_in.at[side], (there, h))
         send(far, (far_s, far_r), list_ref, list_in.at[side], (there, h))
 
+    for copy in small:
+        copy.wait()
     mine = pl.ds(pl.multiple_of(h * part, part), part)
     atom = lax.broadcasted_iota(jnp.int32, (width, 1), 0)
     for b in range(blocks):
@@ -334,7 +344,6 @@
     part = width // peers
     f32, bf16, i32 = jnp.float32, jnp.bfloat16, jnp.int32
     vmem = pl.BlockSpec(memory_space=pltpu.VMEM)
-    smem = pl.BlockSpec(memory_space=pltpu.SMEM)
     hbm = pl.BlockSpec(memory_space=pltpu.HBM)
     dma = pltpu.SemaphoreType.DMA
     near, far, last = 3 * (peers - 1), 2 * half + 6, 2 * (peers - 1)
@@ -345,9 +354,13 @@
             jax.ShapeDtypeStruct((1, atoms), f32),
             jax.ShapeDtypeStruct((1, 128), f32),
         ),
-        in_specs=[smem] * 2 + [hbm] + [vmem] * 3 + [hbm, vmem, hbm],
+        in_specs=[hbm] * 9,
         out_specs=(vmem,) * 3,
         scratch_shapes=[
+            pltpu.SMEM((2, tiles), i32),
+            pltpu.SMEM((1,), i32),
+            pltpu.VMEM((3, atoms), f32),
+            pltpu.VMEM((1, blocks), i32),
             pltpu.VMEM(mix_w.shape, bf16),
             pltpu.VMEM((peers, chans, atoms), bf16),
             pltpu.VMEM((peers, 2 * half, chans, width), bf16),
@@ -367,7 +380,7 @@
             pltpu.VMEM((peers, 8, blocks * part), f32),
             pltpu.VMEM((8, 128), f32),
             pltpu.VMEM((groups, 8, 128), f32),
-            dma((4,)),
+            dma((8,)),
             dma((near,)),
             dma((near,)),
             dma((far,)),
@@ -380,7 +393,7 @@
             dma((groups,)),
         ],
         compiler_params=pltpu.CompilerParams(
-            collective_id=0, has_side_effects=True, vmem_limit_bytes=50 * 1024 * 1024
+            collective_id=0, has_side_effects=True, vmem_limit_bytes=66860000
         ),
         name="layer",
     )(

time: 37.3 us -> 35.6 us (0.954)
  local copies, waits for them, and re-layouts: 4.34 us -> 2.07 us
  Pallas kernels: 30.2 us -> 30.9 us
    unnamed x18 -> x6, local copies, waits for them, and re-layouts: 4.34 us -> 2.07 us
    pallas_call x1, Pallas kernels: 30.2 us -> 30.9 us  [per_device(): pl.pallas_call(functools.partial(layer_kernel, shape, basis_count), out_s...]
where the time goes in v4:
time: 35.6 us; the launch traced here: 35.4 us
  Pallas kernels  30.9 us (87%)
  between operations  2.46 us (7%)
  local copies, waits for them, and re-layouts  2.07 us (6%)
    pallas_call x1, Pallas kernels, per_device(): pl.pallas_call(functools.partial(layer_kernel, shape, basis_count), out_s...  30.9 us
    unnamed x6, local copies, waits for them, and re-layouts  2.07 us

profile of v4, /device:TPU:0, one launch (start us, length us, event | category | flops | bytes accessed | tf_op | source)
XLA Modules:
  0.0 35.4 jit_solution(13345421326222575169)
XLA Ops:
  1.3 30.9 %layer.1 = (bf16[64,512]{1,0:T(8,128)(2,1)}, f32[1,512]{1,0:T(1,128)}, f32[1,128]{1,0:T(1,128)}) custom-call(s32[2,24]{1,0:T(2,128)} %bitcast.12, s32[1]{0:T(128)S(6)} %copy.15.count_ref, bf16[64,512]{1,0:T(8,128)(2,1)} %feat_ref.1, f32[3,512]{1,0:T(4,128)} %where_hbm.1, s32[1,4]{1,0:T(1,128)} %bitcast.14, s32[2,2]{1,0:T(2,128)} %bitcast.13, ...), custom_call_target="tpu_custom_call" | custom-call | tf_op jit(solution)/shard_map/layer/pallas_call | solution.py:350
  32.2 0.0 copy-start
  32.2 1.5 %copy.16 = bf16[64,512]{1,0:T(8,128)(2,1)} copy(bf16[64,512]{1,0:T(8,128)(2,1)} %get-tuple-element.12) | data formatting | bytes 131072
  33.7 0.0 copy-done
  33.7 0.0 copy-start.1
  33.7 0.6 %copy.17 = f32[512]{0:T(512)} copy(f32[512]{0:T(512)S(1)} %bitcast.11) | data formatting | bytes 4096
  34.2 0.0 copy-done.1
Async XLA Ops:
  32.2 1.5 %copy-start = (f32[1,512]{1,0:T(1,128)S(1)}, f32[1,512]{1,0:T(1,128)}, u32[]{:S(2)}) copy-start(f32[1,512]{1,0:T(1,128)} %get-tuple-element.7) | copy-start | bytes 6148
  33.7 0.6 %copy-start.1 = (f32[1,128]{1,0:T(1,128)S(1)}, f32[1,128]{1,0:T(1,128)}, u32[]{:S(2)}) copy-start(f32[1,128]{1,0:T(1,128)} %get-tuple-element.8) | copy-start | bytes 1540

commit v5 on v4

--- a/solution.py
+++ b/solution.py
@@ -393,19 +393,24 @@
             dma((groups,)),
         ],
         compiler_params=pltpu.CompilerParams(
-            collective_id=0, has_side_effects=True, vmem_limit_bytes=66860000
+            collective_id=0, has_side_effects=True, vmem_limit_bytes=50 * 1024 * 1024
         ),
         name="layer",
     )(
-        tile_pairs[0].T,
+        pltpu.with_memory_space_constraint(tile_pairs[0].T, pltpu.HBM),
         tile_count,
-        features,
-        positions,
-        block_counts[None],
-        ghost_lists[0],
-        radial_w.transpose(1, 0, 2),
-        read_w[None],
-        mix_w,
+        *(
+            pltpu.with_memory_space_constraint(value, pltpu.HBM)
+            for value in (
+                features,
+                positions,
+                block_counts[None],
+                ghost_lists[0],
+                radial_w.transpose(1, 0, 2),
+                read_w[None],
+                mix_w,
+            )
+        )
     )
     return updated, energies.reshape(-1), scale[0, 0]
 

time: 35.6 us -> 33.8 us (0.949)
  Pallas kernels: 30.9 us -> 30 us
  local copies, waits for them, and re-layouts: 2.07 us -> 1.21 us
    pallas_call x1, Pallas kernels: 30.9 us -> 30 us  [per_device(): pl.pallas_call(functools.partial(layer_kernel, shape, basis_count), out_s...]
    unnamed x6 -> x2, local copies, waits for them, and re-layouts: 2.07 us -> 1.21 us
where the time goes in v5:
time: 33.8 us; the launch traced here: 33.6 us
  Pallas kernels  30 us (89%)
  between operations  2.45 us (7%)
  local copies, waits for them, and re-layouts  1.21 us (4%)
    pallas_call x1, Pallas kernels, per_device(): pl.pallas_call(functools.partial(layer_kernel, shape, basis_count), out_s...  30 us
    unnamed x2, local copies, waits for them, and re-layouts  1.21 us

profile of v5, /device:TPU:0, one launch (start us, length us, event | category | flops | bytes accessed | tf_op | source)
XLA Modules:
  0.0 33.6 jit_solution(9672907963380844367)
XLA Ops:
  1.3 30.0 %layer.1 = (bf16[64,512]{1,0:T(8,128)(2,1)S(1)}, f32[1,512]{1,0:T(1,128)S(1)}, f32[1,128]{1,0:T(1,128)S(1)}) custom-call(s32[2,24]{1,0:T(2,128)} %bitcast.13, s32[1]{0:T(128)S(6)} %copy.15.count_ref, bf16[64,512]{1,0:T(8,128)(2,1)} %feat_ref.1, f32[3,512]{1,0:T(4,128)} %where_hbm.1, s32[1,4]{1,0:T(1,128)} %bitcast.15, s32[2,2]{1,0:T(2,128)} %bitcast.14, ...), custom_call_target="tpu_custom_call" | custom-call | tf_op jit(solution)/shard_map/layer/pallas_call | solution.py:350
  31.3 0.6 %copy.16 = bf16[64,512]{1,0:T(8,128)(2,1)} copy(bf16[64,512]{1,0:T(8,128)(2,1)S(1)} %get-tuple-element.12) | data formatting | bytes 131072
  31.9 0.6 %copy.17 = f32[512]{0:T(512)} copy(f32[512]{0:T(512)S(1)} %bitcast.10) | data formatting | bytes 4096
